TPU v7x, 8 devices: a whole 2x2x1 slice. The times are simulated.
8 devices in a mesh: dp: 8 (over z, y, x, core).
Axes of the slice: x: 2, y: 2, z: 1, core: 2. Of those that a mesh axis runs over, the one named last changes fastest.
Arguments:
- grad_embed: bfloat16 [8, 2000, 4608], P('dp')
- grad_q: bfloat16 [8, 6, 4608, 32], P('dp')
- grad_k: bfloat16 [8, 6, 4608, 16], P('dp')
- grad_v: bfloat16 [8, 6, 4608, 16], P('dp')
- grad_out: bfloat16 [8, 6, 32, 4608], P('dp')
- grad_gate: bfloat16 [8, 6, 4608, 288], P('dp')
- grad_up: bfloat16 [8, 6, 4608, 288], P('dp')
- grad_down: bfloat16 [8, 6, 288, 4608], P('dp')
- grad_norms: bfloat16 [8, 6, 4, 4608], P('dp')
- grad_qk_norms: bfloat16 [8, 6, 2, 128], P('dp')
- first_moment: float32 [35870208], P('dp')
- second_moment: float32 [35870208], P('dp')
- master_param: float32 [35870208], P('dp')
- hyper_params: float32 [5], replicated
Outputs:
- output 1: bfloat16 [2000, 4608], replicated
- output 2: bfloat16 [6, 4608, 32], replicated
- output 3: bfloat16 [6, 4608, 16], replicated
- output 4: bfloat16 [6, 4608, 16], replicated
- output 5: bfloat16 [6, 32, 4608], replicated
- output 6: bfloat16 [6, 4608, 288], replicated
- output 7: bfloat16 [6, 4608, 288], replicated
- output 8: bfloat16 [6, 288, 4608], replicated
- output 9: bfloat16 [6, 4, 4608], replicated
- output 10: bfloat16 [6, 2, 128], replicated
- output 11: float32 [35870208], P('dp')
- output 12: float32 [35870208], P('dp')
- output 13: float32 [35870208], P('dp')
All inputs are finite; a program needn't handle non-finite values.
Results may differ from a plain program's by a relative error of at most 0.001.
Values are sent between devices in bfloat16 or wider.
A program may use at most 1 GiB of HBM per device.

v0:
```python
import math
import jax
import jax.numpy as jnp
from jax import lax
from jax.sharding import PartitionSpec as P

ADAM_STEP = 7
ADAM_EPS = 1e-8
CLIP_EPS = 1e-6
GRAD_COUNT = 10
NORM_COUNT = 2


def adam_step(grad_part, first_part, second_part, master_part, hyper_params, clip_scale, keep_decay):
    learn_rate = hyper_params[0]
    beta_one = hyper_params[1]
    beta_two = hyper_params[2]
    weight_decay = hyper_params[3]
    clipped = grad_part * clip_scale
    moment_one = beta_one * first_part + (1.0 - beta_one) * clipped
    moment_two = beta_two * second_part + (1.0 - beta_two) * (clipped * clipped)
    m_hat = moment_one / (1.0 - beta_one ** ADAM_STEP)
    v_hat = moment_two / (1.0 - beta_two ** ADAM_STEP)
    direction = m_hat / (jnp.sqrt(v_hat) + ADAM_EPS) + jnp.where(keep_decay, weight_decay * master_part, 0.0)
    new_master = master_part - learn_rate * direction
    return moment_one, moment_two, new_master


def split_params(joined, shapes):
    pieces = []
    start_pos = 0
    for tensor_dims in shapes:
        tensor_size = math.prod(tensor_dims)
        pieces.append(joined[start_pos:start_pos + tensor_size].reshape(tensor_dims))
        start_pos = start_pos + tensor_size
    return pieces


def solution(mesh):
    group_size = mesh.shape["dp"]

    def local_update(*arrays):
        grads = arrays[:GRAD_COUNT]
        first_part, second_part, master_part, hyper_params = arrays[GRAD_COUNT:]
        shapes = [grad_arr.shape[1:] for grad_arr in grads]
        sizes = [math.prod(tensor_dims) for tensor_dims in shapes]
        total_len = sum(sizes)
        shard_len = total_len // group_size
        decay_len = total_len - sum(sizes[GRAD_COUNT - NORM_COUNT:])
        local_vec = jnp.concatenate([grad_arr.reshape(-1) for grad_arr in grads]).reshape(group_size, shard_len)
        received = lax.all_to_all(local_vec, "dp", 0, 0, tiled=True)
        grad_part = jnp.sum(received, axis=0, dtype=jnp.float32) / group_size
        square_sum = lax.psum(jnp.sum(grad_part * grad_part), "dp")
        clip_scale = jnp.minimum(1.0, hyper_params[4] / (jnp.sqrt(square_sum) + CLIP_EPS))
        offset = lax.axis_index("dp") * shard_len
        keep_decay = offset + lax.broadcasted_iota(jnp.int32, (shard_len,), 0) < decay_len
        moment_one, moment_two, new_master = adam_step(grad_part, first_part, second_part, master_part, hyper_params, clip_scale, keep_decay)
        full_vec = lax.all_gather(new_master.astype(jnp.bfloat16), "dp", tiled=True)
        return tuple(split_params(full_vec, shapes)) + (moment_one, moment_two, new_master)

    in_specs = tuple([P("dp")] * GRAD_COUNT + [P("dp"), P("dp"), P("dp"), P()])
    out_specs = tuple([P()] * GRAD_COUNT + [P("dp"), P("dp"), P("dp")])
    return jax.shard_map(local_update, mesh=mesh, in_specs=in_specs, out_specs=out_specs, check_vma=False)
```

profile of v0, /device:TPU:0, one launch (start us, length us, event | category | flops | bytes accessed | tf_op | source)
XLA Modules:
  0.0 4712.4 jit_solution(11443072007970232312)
XLA Ops:
  7.2 33.5 reshape.97
  124.2 41.5 reshape.102
  188.2 41.5 reshape.103
  300.6 885.1 %while.1 = (u32[]{:T(128)}, bf16[35870208]{0:T(1024)(128)(2,1)}, bf16[8,1,4483776]{2,1,0:T(2,128)(2,1)}, u32[]{}, u32[]{}) while((u32[]{:T(128)}, bf16[35870208]{0:T(1024)(128)(2,1)}, bf16[8,1,4483776]{2,1,0:T(2,128)(2,1)}, u32[]{}, u32[]{}) %tuple.32), condition=%wide.cond, body=%wide.body.sunk | while | flops 9 | bytes 44838172
  308.4 103.2 %reshape_dynamic-update-slice_fusion.2 = bf16[8,1,4483776]{2,1,0:T(2,128)(2,1)} fusion(bf16[8,1,4483776]{2,1,0:T(2,128)(2,1)} %get-tuple-element.92, u32[]{:T(128)S(6)} %multiply.19, u32[]{:T(128)S(6)} %multiply.20, bf16[4483776]{0:T(1024)(128)(2,1)S(1)} %dynamic-slice.2), kind=kLoop, calls=%fused_computation.21.clone.1 | loop fusion | bytes 26902920
  419.0 103.2 %reshape_dynamic-update-slice_fusion.2 = bf16[8,1,4483776]{2,1,0:T(2,128)(2,1)} fusion(bf16[8,1,4483776]{2,1,0:T(2,128)(2,1)} %get-tuple-element.92, u32[]{:T(128)S(6)} %multiply.19, u32[]{:T(128)S(6)} %multiply.20, bf16[4483776]{0:T(1024)(128)(2,1)S(1)} %dynamic-slice.2), kind=kLoop, calls=%fused_computation.21.clone.1 | loop fusion | bytes 26902920
  529.6 103.2 %reshape_dynamic-update-slice_fusion.2 = bf16[8,1,4483776]{2,1,0:T(2,128)(2,1)} fusion(bf16[8,1,4483776]{2,1,0:T(2,128)(2,1)} %get-tuple-element.92, u32[]{:T(128)S(6)} %multiply.19, u32[]{:T(128)S(6)} %multiply.20, bf16[4483776]{0:T(1024)(128)(2,1)S(1)} %dynamic-slice.2), kind=kLoop, calls=%fused_computation.21.clone.1 | loop fusion | bytes 26902920
  640.1 103.1 %reshape_dynamic-update-slice_fusion.2 = bf16[8,1,4483776]{2,1,0:T(2,128)(2,1)} fusion(bf16[8,1,4483776]{2,1,0:T(2,128)(2,1)} %get-tuple-element.92, u32[]{:T(128)S(6)} %multiply.19, u32[]{:T(128)S(6)} %multiply.20, bf16[4483776]{0:T(1024)(128)(2,1)S(1)} %dynamic-slice.2), kind=kLoop, calls=%fused_computation.21.clone.1 | loop fusion | bytes 26902920
  750.7 103.2 %reshape_dynamic-update-slice_fusion.2 = bf16[8,1,4483776]{2,1,0:T(2,128)(2,1)} fusion(bf16[8,1,4483776]{2,1,0:T(2,128)(2,1)} %get-tuple-element.92, u32[]{:T(128)S(6)} %multiply.19, u32[]{:T(128)S(6)} %multiply.20, bf16[4483776]{0:T(1024)(128)(2,1)S(1)} %dynamic-slice.2), kind=kLoop, calls=%fused_computation.21.clone.1 | loop fusion | bytes 26902920
  861.3 103.2 %reshape_dynamic-update-slice_fusion.2 = bf16[8,1,4483776]{2,1,0:T(2,128)(2,1)} fusion(bf16[8,1,4483776]{2,1,0:T(2,128)(2,1)} %get-tuple-element.92, u32[]{:T(128)S(6)} %multiply.19, u32[]{:T(128)S(6)} %multiply.20, bf16[4483776]{0:T(1024)(128)(2,1)S(1)} %dynamic-slice.2), kind=kLoop, calls=%fused_computation.21.clone.1 | loop fusion | bytes 26902920
  971.9 103.2 %reshape_dynamic-update-slice_fusion.2 = bf16[8,1,4483776]{2,1,0:T(2,128)(2,1)} fusion(bf16[8,1,4483776]{2,1,0:T(2,128)(2,1)} %get-tuple-element.92, u32[]{:T(128)S(6)} %multiply.19, u32[]{:T(128)S(6)} %multiply.20, bf16[4483776]{0:T(1024)(128)(2,1)S(1)} %dynamic-slice.2), kind=kLoop, calls=%fused_computation.21.clone.1 | loop fusion | bytes 26902920
  1082.5 103.2 %reshape_dynamic-update-slice_fusion.2 = bf16[8,1,4483776]{2,1,0:T(2,128)(2,1)} fusion(bf16[8,1,4483776]{2,1,0:T(2,128)(2,1)} %get-tuple-element.92, u32[]{:T(128)S(6)} %multiply.19, u32[]{:T(128)S(6)} %multiply.20, bf16[4483776]{0:T(1024)(128)(2,1)S(1)} %dynamic-slice.2), kind=kLoop, calls=%fused_computation.21.clone.1 | loop fusion | bytes 26902920
  1186.2 417.1 %reduce.1 = bf16[8,4483776]{1,0:T(8,128)(2,1)} reduce(bf16[8,1,4483776]{2,1,0:T(2,128)(2,1)} %get-tuple-element.43, bf16[]{:T(256)} %broadcast.3), dimensions={1}, to_apply=%get-tuple-element.43.reduce_sub_computation | reduce | bytes 143480832 | tf_op jit(solution)/shard_map/all_to_all | solution.py:51
  1603.3 360.4 %reshape.119 = bf16[8,2,2241888]{2,1,0:T(2,128)(2,1)} reshape(bf16[8,4483776]{1,0:T(8,128)(2,1)} %reduce.1) | data formatting | bytes 143480832
  1978.7 768.8 %all-to-all-done = bf16[8,2,2241888]{2,1,0:T(2,128)(2,1)} async-done(((bf16[8,2,2241888]{2,1,0:T(2,128)(2,1)}), bf16[8,2,2241888]{2,1,0:T(2,128)(2,1)}, u32[]{:S(2)}, u32[]{:S(2)}) %all-to-all-start) | async-done | bytes 71740448 | tf_op jit(solution)/shard_map/all_to_all | solution.py:51
  2747.5 263.5 %reshape.120 = bf16[8,1,4483776]{2,1,0:T(2,128)(2,1)} reshape(bf16[8,2,2241888]{2,1,0:T(2,128)(2,1)} %all-to-all-done) | data formatting | bytes 143480832
  3010.9 377.2 %convert_reduce_fusion = f32[4483776]{0:T(1024)} fusion(bf16[8,1,4483776]{2,1,0:T(2,128)(2,1)} %reshape.120), kind=kLoop, calls=%fused_computation | loop fusion | flops 67256640 | bytes 89675520 | tf_op jit(solution)/shard_map/reduce_sum | solution.py:52
  3421.7 50.0 %fusion = (bf16[4483776]{0:T(1024)(128)(2,1)}, f32[4483776]{0:T(1024)}, f32[4483776]{0:T(1024)}, f32[4483776]{0:T(1024)}) fusion(f32[4483776]{0:T(1024)} %param.26, f32[]{:T(128)} %bitcast.4, s32[]{:T(128)S(6)} %mul.99, f32[]{:T(128)S(6)} %sub.18, f32[]{:T(128)S(6)} %sub.16, f32[]{:T(128)} %bitcast, f32[4483776]{0:T(1024)} %convert_reduce_fusion, ...), kind=kLoop, calls=%fused_computation.16 | loop fusion | flops 89675520 | bytes 134513312 | tf_op jit(solution)/shard_map/convert_element_type | solution.py:58
  3494.0 136.7 %dynamic-update-slice = bf16[35870208]{0:T(1024)(128)(2,1)} dynamic-update-slice(bf16[35870208]{0:T(1024)(128)(2,1)} %broadcast.2, bf16[4483776]{0:T(1024)(128)(2,1)} %get-tuple-element.50, u32[]{:T(128)S(6)} %multiply.8) | dynamic-update-slice | bytes 17935108
  3630.7 798.1 %all-reduce.3.cloned.1.call-done = bf16[35870208]{0:T(1024)(128)(2,1)} async-done(((bf16[35870208]{0:T(1024)(128)(2,1)}), bf16[35870208]{0:T(1024)(128)(2,1)}) %all-reduce.3.cloned.1.call-update) | async-done | bytes 71740432
  4428.7 31.6 fusion.1
  4460.4 38.0 reshape.112
  4521.1 38.0 reshape.113
  4669.8 32.4 reshape.107
  (84 shorter events, 437.6 us)
Async XLA Ops:
  40.7 16.3 copy-start
  61.7 23.1 copy-start.2
  229.7 30.8 copy-start.4
  264.1 19.7 slice-start.4
  267.8 16.0 slice-start.5
  267.8 16.0 slice-start.6
  267.8 16.0 slice-start.7
  267.8 23.9 slice-start
  267.8 23.9 slice-start.1
  283.8 7.9 slice-start.2
  283.8 8.9 slice-start.3
  292.8 6.5 copy-start.1
  1963.7 9.2 copy-start.3
  1963.7 783.8 %all-to-all-start = ((bf16[8,2,2241888]{2,1,0:T(2,128)(2,1)}), bf16[8,2,2241888]{2,1,0:T(2,128)(2,1)}, u32[]{:S(2)}, u32[]{:S(2)}) async-start(bf16[8,2,2241888]{2,1,0:T(2,128)(2,1)} %reshape.119), calls=%async_computation | async-start | bytes 143482880 | tf_op jit(solution)/shard_map/all_to_all | solution.py:51
  1972.9 2455.9 %all-reduce.3.cloned.1.call-start = ((), (), s32[]{:S(2)}) async-start(), calls=%async_computation.1 | async-start | bytes 143482880
Sparse Core Ops, SparseCore 0:
  3630.8 797.8 all-reduce.2
where the time goes:
time: 4750 us; the launch traced here: 4710 us
  local copies, waits for them, and re-layouts  2240 us (47%)
  waiting for transfers between devices  1570 us (33%)
  other arithmetic  854 us (18%)
    unnamed x65, local copies, waits for them, and re-layouts  1850 us
    unnamed x2, waiting for transfers between devices  798 us
    all_to_all x1, waiting for transfers between devices, local_update(): received = lax.all_to_all(local_vec, 'dp', 0, 0, tiled=True)  769 us
    all_to_all x1, other arithmetic, local_update(): received = lax.all_to_all(local_vec, 'dp', 0, 0, tiled=True)  417 us
    reduce_sum x1, other arithmetic, local_update(): grad_part = jnp.sum(received, axis=0, dtype=jnp.float32) / group_size  377 us
    reshape x10, local copies, waits for them, and re-layouts, local_update(): grad_arr.reshape(-1)  176 us
    reshape x9, local copies, waits for them, and re-layouts, split_params(): joined[start_pos:start_pos + tensor_size].reshape(tensor_dims)  158 us
  transfers between devices with their start and end apart: 2, of which 2 were waited for; matrix products, arithmetic and copies ran while one was open for 0% of the time, Pallas kernels for 0%

commit v1 on v0

v1 whole, which is shorter than its diff:
```python
import functools
import math
import jax
import jax.numpy as jnp
from jax import lax
from jax.experimental import pallas as pl
from jax.experimental.pallas import tpu as pltpu
from jax.sharding import PartitionSpec as P

ADAM_STEP = 7
ADAM_EPS = 1e-8
CLIP_EPS = 1e-6
GRAD_COUNT = 10
NORM_COUNT = 2
MESH = pl.DeviceIdType.MESH

GROUP = 8
HALVES = range(2)
OTHERS = range(1, GROUP)
BLK = 36864
ROWS = 288
SHARE = 4483776
HALF = 62
COVER = 2 * HALF
CH = 2
CHUNKS = HALF // CH
AHEAD = 3
SLOTS = 8
OWN = 122
OWN_HALF = OWN // 2
EDGES = (0, 250, 274, 286, 298, 322, 538, 754, 970, 974)
TAIL_BLOCKS = 6
TILE = (36, 8, 128)
COLS = 36
GATHER_CHUNKS = (8, 8, 8, 8, 8, 8, 8, 5)
DECAY_LEN = 970 * BLK


def cover_start(r):
    return (r * SHARE) // BLK


def own_start(r):
    return (r * SHARE + BLK - 1) // BLK


def kind_of(b):
    is_q = (b >= EDGES[1]) & (b < EDGES[2])
    is_kv = (b >= EDGES[2]) & (b < EDGES[4])
    is_gate = (b >= EDGES[5]) & (b < EDGES[7])
    is_row = (b < EDGES[1]) | ((b >= EDGES[4]) & (b < EDGES[5])) | (b >= EDGES[7])
    return is_row, is_gate, is_q, is_kv


def lane_pick(parts, width):
    lane = lax.broadcasted_iota(jnp.int32, parts[0].shape, 1)
    out = parts[0]
    for i in range(1, len(parts)):
        out = jnp.where(lane >= i * width, parts[i], out)
    return out


def roll_to(x, src, dst):
    shift = (dst - src) % 128
    return pltpu.roll(x, shift, 1) if shift else x


def tile_order(kind):
    if kind == "gate":
        return list(range(36))
    if kind == "q":
        return [rt * 9 + ct for ct in range(9) for rt in range(4)]
    return [rt * 18 + ct for ct in range(18) for rt in HALVES]


def pieces(kind):
    out = []
    if kind == "gate":
        for f in range(9):
            for q in range(4):
                k = 4 * f + q
                dd, a = k // 9, k % 9
                out.append(((f, 32, 9), q, (a // 4, dd, 4), a % 4))
    elif kind == "q":
        for ct in range(9):
            for q in range(4):
                out.append(((32 * ct, 32, 1), q, (ct // 4, q, 4), ct % 4))
    else:
        for ct in range(18):
            for q in range(8):
                out.append(((16 * ct, 16, 1), q, (ct // 8, q, 8), ct % 8))
    return out


def width_of(kind):
    return 16 if kind == "kv" else 32


def rows_to_joined(src, dst):
    for i in range(8):
        dst[pl.ds(36 * i, 36), :] = src[:, i, :]


def joined_to_rows(src, emit):
    for t in range(36):
        emit(t, src[pl.ds(t, 8, stride=36), :])


def transposed_to_joined(kind, src, tbuf, dst):
    order = tile_order(kind)
    for j in range(3):
        tiles = [src[t] for t in order[16 * j:16 * j + 16]]
        if len(tiles) < 16:
            tiles.append(jnp.zeros((128 - 8 * len(tiles), 128), jnp.float32))
        tbuf[j] = jnp.concatenate(tiles, axis=0).T
    w = width_of(kind)
    groups = {}
    for drows, dl, srows, sl in pieces(kind):
        groups.setdefault(drows, []).append((dl, srows, sl))
    for (start, count, stride), items in groups.items():
        parts = [None] * (128 // w)
        for dl, (g, s0, sstr), sl in items:
            parts[dl] = roll_to(tbuf[g, pl.ds(s0, count, stride=sstr), :], sl * w, dl * w)
        value = lane_pick(parts, w)
        if stride == 1:
            dst[pl.ds(start, count), :] = value
        else:
            dst[pl.ds(start, count, stride=stride), :] = value


def joined_to_transposed(kind, src, tbuf, emit):
    order = tile_order(kind)
    w = width_of(kind)
    groups = {}
    for drows, dl, srows, sl in pieces(kind):
        groups.setdefault(srows, []).append((sl, drows, dl))
    for (g, s0, sstr), items in groups.items():
        count = items[0][1][1]
        parts = [None] * (128 // w)
        for sl, (start, cnt, stride), dl in items:
            if stride == 1:
                rows = src[pl.ds(start, cnt), :]
            else:
                rows = src[pl.ds(start, cnt, stride=stride), :]
            parts[sl] = roll_to(rows, dl * w, sl * w)
        filler = next(p for p in parts if p is not None)
        parts = [filler if p is None else p for p in parts]
        tbuf[g, pl.ds(s0, count, stride=sstr), :] = lane_pick(parts, w)
    for j in range(3):
        block = tbuf[j].T
        for n, t in enumerate(order[16 * j:16 * j + 16]):
            emit(t, block[8 * n:8 * n + 8, :])


def positions(me):
    y, x, c = me // 4, (me // 2) % 2, me % 2
    xn, yn = 1 - x, 1 - y
    return y, x, c, xn, yn


def dev(y, x, c):
    return (y * 2 + x) * 2 + c


def by_block(b, refs, fn):
    embed, small, gate, up, down, tail = refs
    e = EDGES

    def span(lo, hi, view):
        @pl.when((b >= lo) & (b < hi))
        def _():
            fn(view(b - lo))
    span(0, e[1], lambda n: embed.at[n])
    span(e[1], e[5], lambda n: small.at[n])
    span(e[5], e[6], lambda n: gate.at[n // COLS, :, n % COLS])
    span(e[6], e[7], lambda n: up.at[n // COLS, :, n % COLS])
    span(e[7], e[8], lambda n: down.at[n])
    span(e[8], e[8] + TAIL_BLOCKS, lambda n: tail.at[n])


def reduce_kernel(e_in, q_in, gate_in, up_in, down_in, tail_in, g_hbm, nrm_ref, r1, r2, ld, ld2, st, sbuf, tbuf, fbuf, acc, nbuf,
                  s1_send, s1_recv, s2_send, s2_recv, ld_sem, g_sem, n_send, n_recv):
    me = lax.axis_index("dp")
    y, x, c, xn, yn = positions(me)
    sources = (e_in, q_in, gate_in, up_in, down_in, tail_in)
    barrier = pltpu.get_barrier_semaphore()
    for o in OTHERS:
        pl.semaphore_signal(barrier, inc=1, device_id=((me + o) % GROUP,), device_id_type=MESH)
    pl.semaphore_wait(barrier, GROUP - 1)

    partner = dev(y, x, 1 - c)
    def targets(h):
        cy, cx = (y, xn) if h == 0 else (yn, x)
        oy, ox = (1 - cy, cx) if h == 0 else (cy, 1 - cx)
        py, px = (1 - y, x) if h == 0 else (y, 1 - x)
        return (
            (partner, 0, (dev(py, px, 1 - c), partner)),
            (dev(cy, cx, 0), 1 + c, (dev(oy, ox, 0), dev(cy, cx, 0))),
            (dev(cy, cx, 1), 1 + c, (dev(oy, ox, 1), dev(cy, cx, 1))),
        )

    def send(h, n, t):
        d, k = t // CHUNKS, t % CHUNKS
        device, slot, dests = targets(h)[n]
        dest = dests[0] * (1 - d) + dests[1] * d
        for j in range(CH):
            at = k * CH + j

            def start(src):
                pltpu.make_async_remote_copy(
                    src_ref=src, dst_ref=r1.at[h, slot, d, at],
                    send_sem=s1_send.at[h, n, t % SLOTS], recv_sem=s1_recv.at[h, slot, t],
                    device_id=(device,), device_id_type=MESH).start()
            by_block(cover_start(dest) + h * HALF + at, sources, start)

    def sent(h, n, t):
        view = ld.at[h, 0]
        pltpu.make_async_copy(view, view, s1_send.at[h, n, t % SLOTS]).wait()

    total_steps = 2 * CHUNKS

    def issue(t):
        @pl.when(t < total_steps)
        def _():
            for n in (1, 2, 0):
                for h in HALVES:
                    @pl.when(t >= SLOTS)
                    def _():
                        sent(h, n, t - SLOTS)
                    send(h, n, t)

    def first_issue(t, carry):
        issue(t)
        return carry

    lax.fori_loop(0, AHEAD, first_issue, 0)

    other = (dev(yn, x, c), dev(y, xn, c))

    def wait_stage1(h, t):
        d, k = t // CHUNKS, t % CHUNKS
        for slot in range(3):
            view = r1.at[h, slot, d, pl.ds(k * CH, CH)]
            pltpu.make_async_copy(view, view, s1_recv.at[h, slot, t]).wait()

    def start_loads(h, t, dest):
        d, k = t // CHUNKS, t % CHUNKS
        for j in range(CH):
            def start(src):
                pltpu.make_async_copy(src, ld.at[h, 3, j], ld_sem.at[h, 3]).start()
            by_block(cover_start(dest) + h * HALF + k * CH + j, sources, start)
        for slot in range(3):
            pltpu.make_async_copy(
                r1.at[h, slot, d, pl.ds(k * CH, CH)], ld.at[h, slot], ld_sem.at[h, slot]).start()

    def wait_loads(h):
        for slot in range(4):
            pltpu.make_async_copy(ld.at[h, slot], ld.at[h, slot], ld_sem.at[h, slot]).wait()

    def partial_sum(h, j, t0):
        rows = [ld[h, s, j, pl.ds(t0, 4)].astype(jnp.float32) for s in range(4)]
        return (rows[3] + rows[0]) + (rows[1] + rows[2])

    def stage2_copy(h, k):
        return pltpu.make_async_remote_copy(
            src_ref=st.at[h, k % SLOTS], dst_ref=r2.at[h, pl.ds(k * CH, CH)],
            send_sem=s2_send.at[h, k % SLOTS], recv_sem=s2_recv.at[h, k],
            device_id=(other[h],), device_id_type=MESH)

    def other_step(k, carry):
        issue(k + AHEAD)
        for h in HALVES:
            wait_stage1(h, k)
            start_loads(h, k, other[h])
        for h in HALVES:
            @pl.when(k >= SLOTS)
            def _():
                stage2_copy(h, k - SLOTS).wait_send()
            wait_loads(h)
            for j in range(CH):
                def add(i, z):
                    st[h, k % SLOTS, j, pl.ds(i * 4, 4)] = partial_sum(h, j, i * 4)
                    return z
                lax.fori_loop(0, 9, add, 0)
            stage2_copy(h, k).start()
        return carry

    lax.fori_loop(0, CHUNKS, other_step, 0)

    acc[...] = jnp.zeros_like(acc)
    first, last = own_start(me), own_start(me + 1)

    def g_copy(h, k):
        row = pl.multiple_of((h * HALF + k * CH) * ROWS, 8)
        return pltpu.make_async_copy(
            fbuf.at[h, k % 2], g_hbm.at[pl.ds(row, CH * ROWS)], g_sem.at[h, k % 2])

    def own_step(k, carry):
        t = k + CHUNKS
        issue(t + AHEAD)
        for h in HALVES:
            wait_stage1(h, t)
            view = r2.at[h, pl.ds(k * CH, CH)]
            pltpu.make_async_copy(view, view, s2_recv.at[h, k]).wait()
            start_loads(h, t, me)
            pltpu.make_async_copy(view, ld2.at[h], ld_sem.at[h, 4]).start()
        for h in HALVES:
            @pl.when(k >= 2)
            def _():
                g_copy(h, k - 2).wait()
            wait_loads(h)
            pltpu.make_async_copy(ld2.at[h], ld2.at[h], ld_sem.at[h, 4]).wait()
            for j in range(CH):
                b = cover_start(me) + h * HALF + k * CH + j
                weight = jnp.where((b >= first) & (b < last), 1.0, 0.0)

                def add(i, z):
                    s = partial_sum(h, j, i * 4) + ld2[h, j, pl.ds(i * 4, 4)]
                    sbuf[pl.ds(i * 4, 4)] = s
                    return z + jnp.sum(s * s, axis=0)
                sq = lax.fori_loop(0, 9, add, jnp.zeros((8, 128), jnp.float32))
                acc[...] += sq * weight
                dst = fbuf.at[h, k % 2, pl.ds(j * ROWS, ROWS)]
                is_row, is_gate, is_q, is_kv = kind_of(b)
                pl.when(is_row)(functools.partial(rows_to_joined, sbuf, dst))
                pl.when(is_gate)(functools.partial(transposed_to_joined, "gate", sbuf, tbuf, dst))
                pl.when(is_q)(functools.partial(transposed_to_joined, "q", sbuf, tbuf, dst))
                pl.when(is_kv)(functools.partial(transposed_to_joined, "kv", sbuf, tbuf, dst))
            g_copy(h, k).start()
        return carry

    lax.fori_loop(0, CHUNKS, own_step, 0)

    nbuf[me] = acc[...]

    def norm_copy(o):
        return pltpu.make_async_remote_copy(
            src_ref=acc, dst_ref=nbuf.at[me], send_sem=n_send.at[o - 1], recv_sem=n_recv.at[me],
            device_id=((me + o) % GROUP,), device_id_type=MESH)

    for o in OTHERS:
        norm_copy(o).start()
    for h in HALVES:
        for k in range(CHUNKS - 2, CHUNKS):
            g_copy(h, k).wait()
        for k in range(CHUNKS - SLOTS, CHUNKS):
            stage2_copy(h, k).wait_send()
        for n in range(3):
            for t in range(total_steps - SLOTS, total_steps):
                sent(h, n, t)
    for o in OTHERS:
        peer = (me + o) % GROUP
        pltpu.make_async_copy(nbuf.at[peer], nbuf.at[peer], n_recv.at[peer]).wait()
    for o in OTHERS:
        norm_copy(o).wait_send()
    total = nbuf[0]
    for i in OTHERS:
        total = total + nbuf[i]
    nrm_ref[...] = total


def run_reduce(sources):
    any_spec = pl.BlockSpec(memory_space=pl.ANY)
    f32, bf16 = jnp.float32, jnp.bfloat16
    tile = TILE
    out_shape = (
        jax.ShapeDtypeStruct((COVER * ROWS, 128), f32),
        jax.ShapeDtypeStruct((8, 128), f32),
        jax.ShapeDtypeStruct((2, 3, 2, HALF) + tile, bf16),
        jax.ShapeDtypeStruct((2, HALF) + tile, f32),
    )
    dma = pltpu.SemaphoreType.DMA
    outs = pl.pallas_call(
        reduce_kernel, out_shape=out_shape, in_specs=[any_spec] * len(sources),
        out_specs=(any_spec, pl.BlockSpec(memory_space=pltpu.VMEM), any_spec, any_spec),
        scratch_shapes=[
            pltpu.VMEM((2, 4, CH) + tile, bf16),
            pltpu.VMEM((2, CH) + tile, f32),
            pltpu.VMEM((2, SLOTS, CH) + tile, f32),
            pltpu.VMEM(tile, f32),
            pltpu.VMEM((3, 128, 128), f32),
            pltpu.VMEM((2, 2, CH * ROWS, 128), f32),
            pltpu.VMEM((8, 128), f32),
            pltpu.VMEM((GROUP, 8, 128), f32),
            dma((2, 3, SLOTS)), dma((2, 3, 2 * CHUNKS)), dma((2, SLOTS)), dma((2, CHUNKS)),
            dma((2, 5)), dma((2, 2)), dma((GROUP - 1,)), dma((GROUP,)),
        ],
        compiler_params=pltpu.CompilerParams(collective_id=0, has_side_effects=True),
        name="reduce_scatter",
    )(*sources)
    return outs[0], outs[1]


def update_kernel(me_ref, hyper_ref, nrm_ref, g0, g1, m0, v0, p0, mt, vt, pt,
                  m_out, v_out, p_out, o_ref, gbuf, pbuf, fbuf, tbuf, cbuf):
    i = pl.program_id(0)
    me = me_ref[0]
    lr, b1, b2, wd, max_norm = [hyper_ref[n] for n in range(5)]
    delta = me * SHARE - cover_start(me) * BLK
    rho, odd = delta // 128, me % 2 == 1
    low, high = pl.ds(0, ROWS), pl.ds(ROWS, ROWS)

    def place(buf, at, count, x):
        @pl.when(odd)
        def _():
            buf[pl.ds(at, count), :] = pltpu.roll(x(), 64, 1)

        @pl.when(jnp.logical_not(odd))
        def _():
            buf[pl.ds(at, count), :] = x()

    @pl.when(i == 0)
    def _():
        one = jnp.ones((8, 128), jnp.float32)

        def power(b):
            square = b * b
            cube = b * square
            return cube * (square * square)

        norm = jnp.sqrt(jnp.sum(nrm_ref[...], keepdims=True) * (1.0 / 64.0))
        clip = jnp.minimum(1.0, (one * max_norm) / (norm + CLIP_EPS))
        cbuf[0] = clip * 0.125
        cbuf[1] = one / (one * (1.0 - power(b1)))
        cbuf[2] = one / (one * (1.0 - power(b2)))
        place(gbuf, ROWS, ROWS, lambda: g0[...])

    gbuf[low, :] = gbuf[high, :]
    pbuf[low, :] = pbuf[high, :]
    place(gbuf, ROWS, ROWS, lambda: g1[...])
    size = 32
    scale, inv1, inv2 = [cbuf[n, :1] for n in range(3)]
    lane = lax.broadcasted_iota(jnp.int32, (size, 128), 1)
    sub = lax.broadcasted_iota(jnp.int32, (size, 128), 0)
    own_lane = (lane < 64) | jnp.logical_not(odd)

    def window(buf, row, j):
        at = row + size * j
        return jnp.where(own_lane, buf[pl.ds(at, size), :], buf[pl.ds(at + 1, size), :])

    def run(ms, vs, ps, keep):
        for j in range(ROWS // size):
            part = pl.ds(size * 128 * j, size * 128)
            h = window(gbuf, rho, j) * scale
            m, v, p = [r[part].reshape(size, 128) for r in (ms, vs, ps)]
            m1 = b1 * m + (1.0 - b1) * h
            v1 = b2 * v + (1.0 - b2) * (h * h)
            pos = me * SHARE + i * BLK + size * 128 * j + sub * 128 + lane
            decay = jnp.where(pos < DECAY_LEN, wd * p, 0.0)
            u = (m1 * inv1) / (jnp.sqrt(v1 * inv2) + ADAM_EPS) + decay
            p1 = p - lr * u
            place(pbuf, ROWS + size * j, size, lambda: p1)

            @pl.when(keep)
            def _():
                m_out[part] = m1.reshape(size * 128)
                v_out[part] = v1.reshape(size * 128)
                p_out[part] = p1.reshape(size * 128)

    pl.when(i < 121)(lambda: run(m0, v0, p0, True))
    pl.when(i >= 121)(lambda: run(mt, vt, pt, i < OWN))

    @pl.when(i >= 1)
    def _():
        sigma = (own_start(me) * BLK - me * SHARE) // 128
        for j in range(ROWS // size):
            fbuf[pl.ds(size * j, size), :] = window(pbuf, sigma, j)
        b = own_start(me) + i - 1

        def emit(t, value):
            o_ref[0, t] = value.astype(jnp.bfloat16)
        is_row, is_gate, is_q, is_kv = kind_of(b)
        pl.when(is_row)(functools.partial(joined_to_rows, fbuf, emit))
        pl.when(is_gate)(functools.partial(joined_to_transposed, "gate", fbuf, tbuf, emit))
        pl.when(is_q)(functools.partial(joined_to_transposed, "q", fbuf, tbuf, emit))
        pl.when(is_kv)(functools.partial(joined_to_transposed, "kv", fbuf, tbuf, emit))


def run_update(me, hyper, nrm, g, state, tails):
    f32 = jnp.float32
    flat = lambda f: pl.BlockSpec((BLK,), f)
    main = flat(lambda i, me: (jnp.minimum(i, 120),))
    tail = flat(lambda i, me: (jnp.maximum(i - 121, 0),))
    out = flat(lambda i, me: (jnp.minimum(i, 121),))
    return pl.pallas_call(
        update_kernel,
        grid_spec=pltpu.PrefetchScalarGridSpec(
            num_scalar_prefetch=1, grid=(OWN + 1,),
            in_specs=[
                pl.BlockSpec(memory_space=pltpu.SMEM),
                pl.BlockSpec((8, 128), lambda i, me: (0, 0)),
                pl.BlockSpec((ROWS, 128), lambda i, me: (0, 0)),
                pl.BlockSpec((ROWS, 128), lambda i, me: (i + 1, 0)),
                main, main, main, tail, tail, tail],
            out_specs=[out, out, out,
                       pl.BlockSpec((1, 36, 8, 128), lambda i, me: (me[0] * OWN + jnp.maximum(i - 1, 0), 0, 0, 0))],
            scratch_shapes=[
                pltpu.VMEM((2 * ROWS + 8, 128), f32), pltpu.VMEM((2 * ROWS + 8, 128), f32),
                pltpu.VMEM((ROWS, 128), f32), pltpu.VMEM((3, 128, 128), f32),
                pltpu.VMEM((3, 8, 128), f32)]),
        out_shape=[jax.ShapeDtypeStruct((SHARE,), f32)] * 3
        + [jax.ShapeDtypeStruct((GROUP * OWN, 36, 8, 128), jnp.bfloat16)],
        compiler_params=pltpu.CompilerParams(dimension_semantics=("arbitrary",)),
        name="adam_update",
    )(me, hyper, nrm, g, g, *state, *tails)


def gather_kernel(o_in, o, f_send, f_recv, s_send, s_recv, p_send, p_recv):
    me = lax.axis_index("dp")
    y, x, c, xn, yn = positions(me)
    partner = dev(y, x, 1 - c)
    near = (dev(yn, x, c), dev(y, xn, c))
    far = dev(yn, xn, c)
    barrier = pltpu.get_barrier_semaphore()
    for device in (partner, near[0], near[1]):
        pl.semaphore_signal(barrier, inc=1, device_id=(device,), device_id_type=MESH)
    pl.semaphore_wait(barrier, 3)

    starts = [sum(GATHER_CHUNKS[:n]) for n in range(len(GATHER_CHUNKS))]

    def span(h, share, n):
        return o.at[pl.ds(share * OWN + h * OWN_HALF + starts[n], GATHER_CHUNKS[n])]

    def copy(h, share, n, send, recv, device):
        return pltpu.make_async_remote_copy(
            src_ref=span(h, share, n), dst_ref=span(h, share, n), send_sem=send, recv_sem=recv,
            device_id=(device,), device_id_type=MESH)

    def first_hop(h, n):
        return copy(h, me, n, f_send.at[h, n], f_recv.at[h, n], near[h])

    def second_hop(h, which, n):
        share = (me, near[h])[which]
        return copy(h, share, n, s_send.at[h, which, n], s_recv.at[h, which, n], near[1 - h])

    shares = lambda h: (me, near[h], near[1 - h], far)

    def to_partner(h, which, n):
        return copy(h, shares(h)[which], n, p_send.at[h, which, n], p_recv.at[h, which, n], partner)

    def arrived(h, share, n, sem):
        pltpu.make_async_copy(span(h, share, n), span(h, share, n), sem).wait()

    count = len(GATHER_CHUNKS)
    for n in range(count):
        for h in HALVES:
            first_hop(h, n).start()
            second_hop(h, 0, n).start()
    for n in range(count):
        for h in HALVES:
            to_partner(h, 0, n).start()
    for n in range(count):
        for h in HALVES:
            arrived(h, near[h], n, f_recv.at[h, n])
            second_hop(h, 1, n).start()
            to_partner(h, 1, n).start()
        for h in HALVES:
            arrived(h, near[1 - h], n, s_recv.at[h, 0, n])
            to_partner(h, 2, n).start()
    for n in range(count):
        for h in HALVES:
            arrived(h, far, n, s_recv.at[h, 1, n])
            to_partner(h, 3, n).start()
    ps = dev(y, x, 1 - c)
    pshares = lambda h: (ps, (dev(yn, x, 1 - c), dev(y, xn, 1 - c))[h],
                         (dev(yn, x, 1 - c), dev(y, xn, 1 - c))[1 - h], dev(yn, xn, 1 - c))
    for which in range(4):
        for n in range(count):
            for h in HALVES:
                arrived(h, pshares(h)[which], n, p_recv.at[h, which, n])
                to_partner(h, which, n).wait_send()
    for n in range(count):
        for h in HALVES:
            first_hop(h, n).wait_send()
            for which in HALVES:
                second_hop(h, which, n).wait_send()


def run_gather(o):
    any_spec = pl.BlockSpec(memory_space=pl.ANY)
    dma = pltpu.SemaphoreType.DMA
    count = len(GATHER_CHUNKS)
    return pl.pallas_call(
        gather_kernel, out_shape=jax.ShapeDtypeStruct(o.shape, o.dtype),
        in_specs=[any_spec], out_specs=any_spec, input_output_aliases={0: 0},
        scratch_shapes=[dma((2, count)), dma((2, count)), dma((2, 2, count)), dma((2, 2, count)),
                        dma((2, 4, count)), dma((2, 4, count))],
        compiler_params=pltpu.CompilerParams(collective_id=1, has_side_effects=True),
        name="all_gather",
    )(o)


def pack(grads):
    embed, q, k, v, out, gate, up, down, norms, qk = [g[0] for g in grads]

    def rows(a):
        return a.reshape(-1, 8, COLS, 128).transpose(0, 2, 1, 3)

    def grid(a):
        layers, wide, high = a.shape
        return a.transpose(0, 2, 1).reshape(layers, high // 8, 8, COLS, 128).transpose(0, 1, 3, 2, 4)

    def cols(a, parts):
        a = grid(a)
        a = a.reshape(a.shape[0], a.shape[1], parts, -1, 8, 128).swapaxes(1, 2)
        return a.reshape((-1,) + TILE)

    tail = jnp.concatenate([norms.reshape(-1), qk.reshape(-1)])
    tail = jnp.pad(tail, (0, TAIL_BLOCKS * BLK - tail.shape[0]))
    small = jnp.concatenate([cols(q, 4), cols(k, 2), cols(v, 2), rows(out)])
    return rows(embed), small, grid(gate), grid(up), rows(down), rows(tail.reshape(-1, 4608))


def block_runs(b0, b1):
    cuts = [own_start(r) for r in range(GROUP + 1)]
    out = []
    for r in range(GROUP):
        lo, hi = max(b0, cuts[r]), min(b1, cuts[r + 1])
        if lo < hi:
            out.append((r * OWN + lo - cuts[r], hi - lo))
    return out


def unpack_kernel(o, embed, q, k, v, out, gate, up, down, tail, buf, in_sem, out_sem):
    def rows_out(ref, first):
        def store(slot, count):
            pltpu.make_async_copy(
                buf.at[slot, pl.ds(0, count)], ref.at[pl.ds(first, count)], out_sem.at[slot]).start()
        return store

    def grid_out(ref, layer):
        def store(slot, count):
            def one(rt, z):
                pltpu.make_async_copy(buf.at[slot, :, rt], ref.at[layer, rt], out_sem.at[slot]).start()
                return z
            lax.fori_loop(0, COLS, one, 0)
        return store

    def cols_out(ref, parts):
        high, wide = ref.shape[1], COLS // parts

        def store(slot, count):
            def one(n, z):
                for rt in range(high):
                    pltpu.make_async_copy(
                        buf.at[slot, n, pl.ds(wide * rt, wide)],
                        ref.at[n // parts, rt, pl.ds((n % parts) * wide, wide)], out_sem.at[slot]).start()
                return z
            lax.fori_loop(0, count, one, 0)
        return store

    jobs = []

    def add_rows(ref, b0, b1):
        for lo in range(b0, b1, COLS):
            hi = min(lo + COLS, b1)
            jobs.append((lo, hi - lo, rows_out(ref, lo - b0)))

    e = EDGES
    add_rows(embed, e[0], e[1])
    for layer in range(gate.shape[0]):
        jobs.append((e[5] + COLS * layer, COLS, grid_out(gate, layer)))
        jobs.append((e[6] + COLS * layer, COLS, grid_out(up, layer)))
    jobs.append((e[1], e[2] - e[1], cols_out(q, 4)))
    jobs.append((e[2], e[3] - e[2], cols_out(k, 2)))
    jobs.append((e[3], e[4] - e[3], cols_out(v, 2)))
    add_rows(out, e[4], e[5])
    add_rows(down, e[7], e[8])
    add_rows(tail, e[8], e[9])
    depth = buf.shape[0]

    def load(n):
        b0, count, _ = jobs[n]
        at = 0
        for first, size in block_runs(b0, b0 + count):
            pltpu.make_async_copy(
                o.at[pl.ds(first, size)], buf.at[n % depth, pl.ds(at, size)], in_sem.at[n % depth]).start()
            at += size

    def wait(n, sem):
        view = buf.at[n % depth, pl.ds(0, jobs[n][1])]
        pltpu.make_async_copy(view, view, sem.at[n % depth]).wait()

    lead = depth // 2
    for n in range(len(jobs) + lead):
        if n < len(jobs):
            if n >= depth:
                wait(n - depth, out_sem)
            load(n)
        if n >= lead:
            wait(n - lead, in_sem)
            jobs[n - lead][2]((n - lead) % depth, jobs[n - lead][1])
    for n in range(len(jobs) - depth, len(jobs)):
        wait(n, out_sem)


def run_unpack(o, shapes):
    e, bf16 = EDGES, jnp.bfloat16
    any_spec = pl.BlockSpec(memory_space=pl.ANY)

    def rows(n):
        return (n,) + TILE

    def grid(shape):
        return (shape[0], shape[2] // 8) + TILE
    views = [rows(e[1]), grid(shapes[1]), grid(shapes[2]), grid(shapes[3]), rows(e[5] - e[4]),
             grid(shapes[5]), grid(shapes[6]), rows(e[8] - e[7]), rows(e[9] - e[8])]
    dma = pltpu.SemaphoreType.DMA
    depth = 6
    outs = pl.pallas_call(
        unpack_kernel, out_shape=[jax.ShapeDtypeStruct(s, bf16) for s in views],
        in_specs=[any_spec], out_specs=[any_spec] * len(views),
        scratch_shapes=[pltpu.VMEM((depth, COLS) + TILE, bf16), dma((depth,)), dma((depth,))],
        name="unpack",
    )(o)

    def from_rows(a, shape):
        return a.swapaxes(1, 2).reshape(shape)

    def from_grid(a, shape):
        layers, wide, high = shape
        return a.swapaxes(2, 3).reshape(layers, high, wide).swapaxes(1, 2)
    params = [(from_grid if len(a.shape) > 4 else from_rows)(a, s) for a, s in zip(outs[:8], shapes)]
    tail = from_rows(outs[8], (-1,))
    size = math.prod(shapes[8])
    params.append(tail[:size].reshape(shapes[8]))
    params.append(tail[size:size + math.prod(shapes[9])].reshape(shapes[9]))
    return tuple(params)


def solution(mesh):
    group_size = mesh.shape["dp"]
    assert group_size == GROUP

    def local_update(*arrays):
        grads = arrays[:GRAD_COUNT]
        first_part, second_part, master_part, hyper_params = arrays[GRAD_COUNT:]
        state = (first_part, second_part, master_part)
        shapes = [grad_arr.shape[1:] for grad_arr in grads]
        me = lax.axis_index("dp").astype(jnp.int32).reshape(1)

        heads = jnp.concatenate([s[:BLK] for s in state])
        heads = lax.ppermute(heads, "dp", [(r + 1, r) for r in range(GROUP - 1)])
        rest = 2 * BLK - (SHARE - 121 * BLK) - BLK
        tails = [jnp.concatenate([s[121 * BLK:], heads[n * BLK:(n + 1) * BLK], jnp.zeros((rest,), s.dtype)])
                 for n, s in enumerate(state)]

        g, nrm = run_reduce(pack(grads))
        m1, v1, p1, o = run_update(me, hyper_params, nrm, g, state, tails)
        params = run_unpack(run_gather(o), shapes)
        return params + (m1, v1, p1)

    in_specs = tuple([P("dp")] * GRAD_COUNT + [P("dp"), P("dp"), P("dp"), P()])
    out_specs = tuple([P()] * GRAD_COUNT + [P("dp"), P("dp"), P("dp")])
    return jax.shard_map(local_update, mesh=mesh, in_specs=in_specs, out_specs=out_specs, check_vma=False)
```

time: 4750 us -> 1160 us (0.24)
  local copies, waits for them, and re-layouts: 2240 us -> 22.4 us
  waiting for transfers between devices: 1570 us -> 0.01 us
  Pallas kernels: 0 us -> 1130 us
  other arithmetic: 854 us -> 4.32 us
    unnamed x65 -> x0, local copies, waits for them, and re-layouts: 1850 us -> none
    pallas_call x0 -> x4, Pallas kernels: none -> 1130 us  [the longest x1 605 us: run_reduce(): pl.pallas_call(reduce_kernel, out_shape=out_shape, in_specs=[any_spec] *...]
    unnamed x2 -> x0, waiting for transfers between devices: 798 us -> none
    all_to_all x1 -> x0, waiting for transfers between devices: 769 us -> none  [local_update(): received = lax.all_to_all(local_vec, 'dp', 0, 0, tiled=True)]
    all_to_all x1 -> x0, other arithmetic: 417 us -> none  [local_update(): received = lax.all_to_all(local_vec, 'dp', 0, 0, tiled=True)]
    reduce_sum x2 -> x0, other arithmetic: 387 us -> none  [the longest x1 377 us: local_update(): grad_part = jnp.sum(received, axis=0, dtype=jnp.float32) / group_size]
    reshape x19 -> x1, local copies, waits for them, and re-layouts: 334 us -> 0.76 us  [run_unpack(): params.append(tail[:size].reshape(shapes[8]))]
    convert_element_type x1 -> x0, other arithmetic: 50 us -> none  [local_update(): full_vec = lax.all_gather(new_master.astype(jnp.bfloat16), 'dp', tiled=True)]
  transfers between devices with their start and end apart: 2 -> 1, of which waited for: 2 -> 0; matrix products, arithmetic and copies ran while one was open for 0% -> 1% of each run, Pallas kernels for 0% -> 0%
where the time goes in v1:
time: 1160 us
  Pallas kernels  1130 us (97%)
  local copies, waits for them, and re-layouts  22.4 us (2%)
    pallas_call x1, Pallas kernels, run_reduce(): pl.pallas_call(reduce_kernel, out_shape=out_shape, in_specs=[any_spec] *...  605 us
    pallas_call x1, Pallas kernels, run_gather(): pl.pallas_call(gather_kernel, out_shape=jax.ShapeDtypeStruct(o.shape, o.d...  368 us
    pallas_call x1, Pallas kernels, run_update(): pl.pallas_call(update_kernel, grid_spec=pltpu.PrefetchScalarGridSpec(num_...  107 us
    pallas_call x1, Pallas kernels, run_unpack(): pl.pallas_call(unpack_kernel, out_shape=[jax.ShapeDtypeStruct(s, bf16) fo...  46.8 us
  transfers between devices with their start and end apart: 1, of which 0 were waited for; matrix products, arithmetic and copies ran while one was open for 1% of the time, Pallas kernels for 0%

profile of v1, /device:TPU:0, one launch (start us, length us, event | category | flops | bytes accessed | tf_op | source)
XLA Modules:
  0.0 1156.0 jit_solution(17575654165184953886)
XLA Ops:
  0.6 0.9 slice.38
  1.6 0.9 slice.39
  2.5 0.9 slice.40
  3.5 1.3 collective-permute-start
  4.8 0.7 reshape_squeeze.19
  5.5 1.0 reshape_squeeze.18
  6.5 0.1 reshape_reshape.3
  6.6 0.8 copy.35
  7.4 1.2 copy.29
  8.7 1.2 copy.30
  9.9 1.7 copy.28
  11.6 4.3 pad_maximum_fusion.q_in
  15.8 604.8 %reduce_scatter.1 = (f32[35712,128]{1,0:T(8,128)}, f32[8,128]{1,0:T(8,128)}, bf16[2,3,2,62,36,8,128]{6,5,4,3,2,1,0:T(8,128)(2,1)}, f32[2,62,36,8,128]{4,3,2,1,0:T(8,128)}) custom-call(bf16[250,36,8,128]{3,2,1,0:T(8,128)(2,1)} %bitcast.98, bf16[72,36,8,128]{3,2,1,0:T(8,128)(2,1)} %pad_maximum_fusion.q_in, bf16[6,36,36,8,128]{4,3,2,1,0:T(8,128)(2,1)} %bitcast.99, ...), custom_call_target="tpu_custom_call" | custom-call | tf_op jit(solution)/shard_map/reduce_scatter/pallas_call | solution.py:373
  620.8 3.2 concatenate.23.pt
  623.9 3.1 concatenate.22.vt
  627.1 3.1 concatenate.21.mt
  630.2 107.5 %adam_update.1 = (f32[4483776]{0:T(1024)}, f32[4483776]{0:T(1024)}, f32[4483776]{0:T(1024)}, bf16[976,36,8,128]{3,2,1,0:T(8,128)(2,1)}) custom-call(s32[1]{0:T(128)} %bitcast.me_ref, f32[5]{0:T(128)} %hyper_ref.1, f32[8,128]{1,0:T(8,128)} %get-tuple-element.28.nrm_ref, f32[35712,128]{1,0:T(8,128)} %get-tuple-element.29.g0.g1, ...), custom_call_target="tpu_custom_call" | custom-call | tf_op jit(solution)/shard_map/adam_update/pallas_call | solution.py:485
  737.7 368.1 %all_gather.1.o = bf16[976,36,8,128]{3,2,1,0:T(8,128)(2,1)} custom-call(bf16[976,36,8,128]{3,2,1,0:T(8,128)(2,1)} %get-tuple-element.30.o_in), custom_call_target="tpu_custom_call", output_to_operand_aliasing={{}: (0, {})} | custom-call | tf_op jit(solution)/shard_map/all_gather/pallas_call | solution.py:583
  1105.8 46.8 %unpack.1 = (bf16[250,36,8,128]{3,2,1,0:T(8,128)(2,1)}, bf16[6,4,36,8,128]{4,3,2,1,0:T(8,128)(2,1)}, bf16[6,2,36,8,128]{4,3,2,1,0:T(8,128)(2,1)}, bf16[6,2,36,8,...) custom-call(bf16[976,36,8,128]{3,2,1,0:T(8,128)(2,1)} %all_gather.1.o), custom_call_target="tpu_custom_call" | custom-call | tf_op jit(solution)/shard_map/unpack/pallas_call | solution.py:710
  1152.6 1.0 slice.52
  1153.5 1.0 copy.33
  1154.6 0.8 reshape.115
  1155.4 0.1 slice.47
  1155.5 0.6 slice.53
  (12 shorter events, 0.2 us)
Async XLA Ops:
  3.5 617.2 %collective-permute-start = (f32[110592]{0:T(1024)S(1)}, f32[110592]{0:T(1024)S(1)}, u32[]{:S(2)}, u32[]{:S(2)}) collective-permute-start(f32[110592]{0:T(1024)S(1)} %pad_maximum_fusion.1), channel_id=1, source_target_pairs={{1,0},{2,1},{3,2},{4,3},{5,4},{6,5},{7,6}} | collective-permute-start | bytes 1327112 | tf_op jit(solution)/shard_map/ppermute | solution.py:743
  15.8 604.9 %slice-start.2 = ((f32[4483776]{0:T(1024)}), f32[23232]{0:T(1024)S(1)}, s32[]{:S(2)}) async-start(f32[4483776]{0:T(1024)} %p0.1), calls=%async_computation.2 | async-start | bytes 188416 | tf_op jit(solution)/shard_map/slice | solution.py:745
  15.8 608.1 %slice-start.1 = ((f32[4483776]{0:T(1024)}), f32[23232]{0:T(1024)S(1)}, s32[]{:S(2)}) async-start(f32[4483776]{0:T(1024)} %v0.1), calls=%async_computation.1 | async-start | bytes 188416 | tf_op jit(solution)/shard_map/slice | solution.py:745
  15.8 611.2 %slice-start = ((f32[4483776]{0:T(1024)}), f32[23232]{0:T(1024)S(1)}, s32[]{:S(2)}) async-start(f32[4483776]{0:T(1024)} %m0.1), calls=%async_computation | async-start | bytes 188416 | tf_op jit(solution)/shard_map/slice | solution.py:745

commit v2 on v1

--- a/solution.py
+++ b/solution.py
@@ -15,8 +15,11 @@
 MESH = pl.DeviceIdType.MESH
 
 GROUP = 8
-HALVES = range(2)
+PAIR = 2
+HALVES = range(PAIR)
 OTHERS = range(1, GROUP)
+STATE = range(3)
+ALL = range(4)
 BLK = 36864
 ROWS = 288
 SHARE = 4483776
@@ -32,7 +35,8 @@
 TAIL_BLOCKS = 6
 TILE = (36, 8, 128)
 COLS = 36
-GATHER_CHUNKS = (8, 8, 8, 8, 8, 8, 8, 5)
+NEAR_LAG = 2
+FAR_LAG = 4
 DECAY_LEN = 970 * BLK
 
 
@@ -345,7 +349,7 @@
             g_copy(h, k).wait()
         for k in range(CHUNKS - SLOTS, CHUNKS):
             stage2_copy(h, k).wait_send()
-        for n in range(3):
+        for n in STATE:
             for t in range(total_steps - SLOTS, total_steps):
                 sent(h, n, t)
     for o in OTHERS:
@@ -382,8 +386,8 @@
             pltpu.VMEM((2, 2, CH * ROWS, 128), f32),
             pltpu.VMEM((8, 128), f32),
             pltpu.VMEM((GROUP, 8, 128), f32),
-            dma((2, 3, SLOTS)), dma((2, 3, 2 * CHUNKS)), dma((2, SLOTS)), dma((2, CHUNKS)),
-            dma((2, 5)), dma((2, 2)), dma((GROUP - 1,)), dma((GROUP,)),
+            dma((PAIR, 3, SLOTS)), dma((PAIR, 3, 2 * CHUNKS)), dma((PAIR, SLOTS)), dma((PAIR, CHUNKS)),
+            dma((PAIR, 5)), dma((PAIR, 2)), dma((GROUP - 1,)), dma((GROUP,)),
         ],
         compiler_params=pltpu.CompilerParams(collective_id=0, has_side_effects=True),
         name="reduce_scatter",
@@ -391,203 +395,265 @@
     return outs[0], outs[1]
 
 
-def update_kernel(me_ref, hyper_ref, nrm_ref, g0, g1, m0, v0, p0, mt, vt, pt,
-                  m_out, v_out, p_out, o_ref, gbuf, pbuf, fbuf, tbuf, cbuf):
-    i = pl.program_id(0)
-    me = me_ref[0]
-    lr, b1, b2, wd, max_norm = [hyper_ref[n] for n in range(5)]
-    delta = me * SHARE - cover_start(me) * BLK
-    rho, odd = delta // 128, me % 2 == 1
-    low, high = pl.ds(0, ROWS), pl.ds(ROWS, ROWS)
-
-    def place(buf, at, count, x):
-        @pl.when(odd)
-        def _():
-            buf[pl.ds(at, count), :] = pltpu.roll(x(), 64, 1)
-
-        @pl.when(jnp.logical_not(odd))
-        def _():
-            buf[pl.ds(at, count), :] = x()
-
-    @pl.when(i == 0)
-    def _():
-        one = jnp.ones((8, 128), jnp.float32)
-
-        def power(b):
-            square = b * b
-            cube = b * square
-            return cube * (square * square)
-
-        norm = jnp.sqrt(jnp.sum(nrm_ref[...], keepdims=True) * (1.0 / 64.0))
-        clip = jnp.minimum(1.0, (one * max_norm) / (norm + CLIP_EPS))
-        cbuf[0] = clip * 0.125
-        cbuf[1] = one / (one * (1.0 - power(b1)))
-        cbuf[2] = one / (one * (1.0 - power(b2)))
-        place(gbuf, ROWS, ROWS, lambda: g0[...])
-
-    gbuf[low, :] = gbuf[high, :]
-    pbuf[low, :] = pbuf[high, :]
-    place(gbuf, ROWS, ROWS, lambda: g1[...])
-    size = 32
-    scale, inv1, inv2 = [cbuf[n, :1] for n in range(3)]
-    lane = lax.broadcasted_iota(jnp.int32, (size, 128), 1)
-    sub = lax.broadcasted_iota(jnp.int32, (size, 128), 0)
-    own_lane = (lane < 64) | jnp.logical_not(odd)
-
-    def window(buf, row, j):
-        at = row + size * j
-        return jnp.where(own_lane, buf[pl.ds(at, size), :], buf[pl.ds(at + 1, size), :])
-
-    def run(ms, vs, ps, keep):
-        for j in range(ROWS // size):
-            part = pl.ds(size * 128 * j, size * 128)
-            h = window(gbuf, rho, j) * scale
-            m, v, p = [r[part].reshape(size, 128) for r in (ms, vs, ps)]
-            m1 = b1 * m + (1.0 - b1) * h
-            v1 = b2 * v + (1.0 - b2) * (h * h)
-            pos = me * SHARE + i * BLK + size * 128 * j + sub * 128 + lane
-            decay = jnp.where(pos < DECAY_LEN, wd * p, 0.0)
-            u = (m1 * inv1) / (jnp.sqrt(v1 * inv2) + ADAM_EPS) + decay
-            p1 = p - lr * u
-            place(pbuf, ROWS + size * j, size, lambda: p1)
-
-            @pl.when(keep)
-            def _():
-                m_out[part] = m1.reshape(size * 128)
-                v_out[part] = v1.reshape(size * 128)
-                p_out[part] = p1.reshape(size * 128)
-
-    pl.when(i < 121)(lambda: run(m0, v0, p0, True))
-    pl.when(i >= 121)(lambda: run(mt, vt, pt, i < OWN))
-
-    @pl.when(i >= 1)
-    def _():
-        sigma = (own_start(me) * BLK - me * SHARE) // 128
-        for j in range(ROWS // size):
-            fbuf[pl.ds(size * j, size), :] = window(pbuf, sigma, j)
-        b = own_start(me) + i - 1
-
-        def emit(t, value):
-            o_ref[0, t] = value.astype(jnp.bfloat16)
-        is_row, is_gate, is_q, is_kv = kind_of(b)
-        pl.when(is_row)(functools.partial(joined_to_rows, fbuf, emit))
-        pl.when(is_gate)(functools.partial(joined_to_transposed, "gate", fbuf, tbuf, emit))
-        pl.when(is_q)(functools.partial(joined_to_transposed, "q", fbuf, tbuf, emit))
-        pl.when(is_kv)(functools.partial(joined_to_transposed, "kv", fbuf, tbuf, emit))
-
-
-def run_update(me, hyper, nrm, g, state, tails):
-    f32 = jnp.float32
-    flat = lambda f: pl.BlockSpec((BLK,), f)
-    main = flat(lambda i, me: (jnp.minimum(i, 120),))
-    tail = flat(lambda i, me: (jnp.maximum(i - 121, 0),))
-    out = flat(lambda i, me: (jnp.minimum(i, 121),))
-    return pl.pallas_call(
-        update_kernel,
-        grid_spec=pltpu.PrefetchScalarGridSpec(
-            num_scalar_prefetch=1, grid=(OWN + 1,),
-            in_specs=[
-                pl.BlockSpec(memory_space=pltpu.SMEM),
-                pl.BlockSpec((8, 128), lambda i, me: (0, 0)),
-                pl.BlockSpec((ROWS, 128), lambda i, me: (0, 0)),
-                pl.BlockSpec((ROWS, 128), lambda i, me: (i + 1, 0)),
-                main, main, main, tail, tail, tail],
-            out_specs=[out, out, out,
-                       pl.BlockSpec((1, 36, 8, 128), lambda i, me: (me[0] * OWN + jnp.maximum(i - 1, 0), 0, 0, 0))],
-            scratch_shapes=[
-                pltpu.VMEM((2 * ROWS + 8, 128), f32), pltpu.VMEM((2 * ROWS + 8, 128), f32),
-                pltpu.VMEM((ROWS, 128), f32), pltpu.VMEM((3, 128, 128), f32),
-                pltpu.VMEM((3, 8, 128), f32)]),
-        out_shape=[jax.ShapeDtypeStruct((SHARE,), f32)] * 3
-        + [jax.ShapeDtypeStruct((GROUP * OWN, 36, 8, 128), jnp.bfloat16)],
-        compiler_params=pltpu.CompilerParams(dimension_semantics=("arbitrary",)),
-        name="adam_update",
-    )(me, hyper, nrm, g, g, *state, *tails)
-
-
-def gather_kernel(o_in, o, f_send, f_recv, s_send, s_recv, p_send, p_recv):
+def update_kernel(hyper_ref, nrm_ref, g_hbm, m_hbm, v_hbm, p_hbm, mt, vt, pt,
+                  m_out, v_out, p_out, o, gbuf, pbuf, fbuf, tbuf, cbuf, gin, sin, sout, obuf,
+                  in_sem, out_sem, o_sem, f_send, f_recv, s_send, s_recv, p_send, p_recv):
     me = lax.axis_index("dp")
     y, x, c, xn, yn = positions(me)
     partner = dev(y, x, 1 - c)
     near = (dev(yn, x, c), dev(y, xn, c))
     far = dev(yn, xn, c)
     barrier = pltpu.get_barrier_semaphore()
-    for device in (partner, near[0], near[1]):
+    for device in (partner,) + near:
         pl.semaphore_signal(barrier, inc=1, device_id=(device,), device_id_type=MESH)
     pl.semaphore_wait(barrier, 3)
 
-    starts = [sum(GATHER_CHUNKS[:n]) for n in range(len(GATHER_CHUNKS))]
-
-    def span(h, share, n):
-        return o.at[pl.ds(share * OWN + h * OWN_HALF + starts[n], GATHER_CHUNKS[n])]
-
-    def copy(h, share, n, send, recv, device):
-        return pltpu.make_async_remote_copy(
-            src_ref=span(h, share, n), dst_ref=span(h, share, n), send_sem=send, recv_sem=recv,
-            device_id=(device,), device_id_type=MESH)
-
-    def first_hop(h, n):
-        return copy(h, me, n, f_send.at[h, n], f_recv.at[h, n], near[h])
-
-    def second_hop(h, which, n):
+    lr, b1, b2, wd, max_norm = [hyper_ref[n] for n in range(5)]
+    delta = me * SHARE - cover_start(me) * BLK
+    rho, odd = delta // 128, me % 2 == 1
+    sigma = (own_start(me) * BLK - me * SHARE) // 128
+    low, high = pl.ds(0, ROWS), pl.ds(ROWS, ROWS)
+    state, tails, outs = (m_hbm, v_hbm, p_hbm), (mt, vt, pt), (m_out, v_out, p_out)
+    size = 32
+    lane = lax.broadcasted_iota(jnp.int32, (size, 128), 1)
+    sub = lax.broadcasted_iota(jnp.int32, (size, 128), 0)
+    own_lane = (lane < 64) | jnp.logical_not(odd)
+
+    def place(buf, at, count, value):
+        @pl.when(odd)
+        def _():
+            buf[pl.ds(at, count), :] = pltpu.roll(value(), 64, 1)
+
+        @pl.when(jnp.logical_not(odd))
+        def _():
+            buf[pl.ds(at, count), :] = value()
+
+    def window(buf, row, j):
+        at = row + size * j
+        return jnp.where(own_lane, buf[pl.ds(at, size), :], buf[pl.ds(at + 1, size), :])
+
+    def flat(i, n, first=0, count=BLK):
+        return pl.ds(pl.multiple_of((i % 2 * 3 + n) * BLK + first, 1024), count)
+
+    def span(i):
+        return pl.ds(pl.multiple_of(i * BLK, 1024), BLK)
+
+    def g_copy(i, slot):
+        rows = pl.ds(pl.multiple_of(i * ROWS, 8), ROWS)
+        return pltpu.make_async_copy(g_hbm.at[rows], gin.at[slot], in_sem.at[slot, 3])
+
+    def start_loads(i):
+        g_copy(i + 1, i % 2).start()
+        for n in STATE:
+            @pl.when(i < OWN - 1)
+            def _():
+                pltpu.make_async_copy(state[n].at[span(i)], sin.at[flat(i, n)], in_sem.at[i % 2, n]).start()
+
+            @pl.when(i >= OWN - 1)
+            def _():
+                pltpu.make_async_copy(
+                    tails[n].at[span(i - OWN + 1)], sin.at[flat(i, n)], in_sem.at[i % 2, n]).start()
+
+    def store_copy(i, n):
+        return pltpu.make_async_copy(sout.at[flat(i, n)], outs[n].at[span(i)], out_sem.at[i % 2, n])
+
+    def block_copy(j):
+        return pltpu.make_async_copy(
+            obuf.at[j % SLOTS], o.at[me * OWN_HALF + j // 2, j % 2], o_sem.at[j % SLOTS])
+
+    def step(i):
+        @pl.when(i < OWN)
+        def _():
+            start_loads(i + 1)
+        g_copy(i + 1, i % 2).wait()
+        for n in STATE:
+            view = sin.at[flat(i, n)]
+            pltpu.make_async_copy(view, view, in_sem.at[i % 2, n]).wait()
+
+            @pl.when((i >= 2) & (i < OWN))
+            def _():
+                store_copy(i - 2, n).wait()
+        gbuf[low, :] = gbuf[high, :]
+        pbuf[low, :] = pbuf[high, :]
+        place(gbuf, ROWS, ROWS, lambda: gin[i % 2])
+        scale, inv1, inv2 = [cbuf[n, :1] for n in STATE]
+        keep = i < OWN
+        for j in range(ROWS // size):
+            first, count = size * 128 * j, size * 128
+            h = window(gbuf, rho, j) * scale
+            m, v, p = [sin[flat(i, n, first, count)].reshape(size, 128) for n in STATE]
+            m1 = b1 * m + (1.0 - b1) * h
+            v1 = b2 * v + (1.0 - b2) * (h * h)
+            pos = me * SHARE + i * BLK + first + sub * 128 + lane
+            decay = jnp.where(pos < DECAY_LEN, wd * p, 0.0)
+            u = (m1 * inv1) / (jnp.sqrt(v1 * inv2) + ADAM_EPS) + decay
+            p1 = p - lr * u
+            place(pbuf, ROWS + size * j, size, lambda: p1)
+
+            @pl.when(keep)
+            def _():
+                for n, value in enumerate((m1, v1, p1)):
+                    sout[flat(i, n, first, count)] = value.reshape(count)
+
+        @pl.when(keep)
+        def _():
+            for n in STATE:
+                store_copy(i, n).start()
+
+    def finish(i):
+        j = i - 1
+        for k in range(ROWS // size):
+            fbuf[pl.ds(size * k, size), :] = window(pbuf, sigma, k)
+        b = own_start(me) + j
+
+        def emit(t, value):
+            obuf[j % SLOTS, t] = value.astype(jnp.bfloat16)
+        is_row, is_gate, is_q, is_kv = kind_of(b)
+        pl.when(is_row)(functools.partial(joined_to_rows, fbuf, emit))
+        pl.when(is_gate)(functools.partial(joined_to_transposed, "gate", fbuf, tbuf, emit))
+        pl.when(is_q)(functools.partial(joined_to_transposed, "q", fbuf, tbuf, emit))
+        pl.when(is_kv)(functools.partial(joined_to_transposed, "kv", fbuf, tbuf, emit))
+        block_copy(j).start()
+
+    def view(h, share, q, count):
+        return o.at[pl.ds(share * OWN_HALF + q * CH, count), h]
+
+    def copy(h, share, q, count, send, recv, device):
+        span_ = view(h, share, q, count)
+        pltpu.make_async_remote_copy(
+            src_ref=span_, dst_ref=span_, send_sem=send, recv_sem=recv,
+            device_id=(device,), device_id_type=MESH).start()
+
+    def to_partner(h, which, q, count):
+        share = (me, near[h], near[1 - h], far)[which]
+        copy(h, share, q, count, p_send.at[h, which], p_recv.at[h, which, q], partner)
+
+    def second_hop(h, which, q, count):
         share = (me, near[h])[which]
-        return copy(h, share, n, s_send.at[h, which, n], s_recv.at[h, which, n], near[1 - h])
-
-    shares = lambda h: (me, near[h], near[1 - h], far)
-
-    def to_partner(h, which, n):
-        return copy(h, shares(h)[which], n, p_send.at[h, which, n], p_recv.at[h, which, n], partner)
-
-    def arrived(h, share, n, sem):
-        pltpu.make_async_copy(span(h, share, n), span(h, share, n), sem).wait()
-
-    count = len(GATHER_CHUNKS)
-    for n in range(count):
-        for h in HALVES:
-            first_hop(h, n).start()
-            second_hop(h, 0, n).start()
-    for n in range(count):
-        for h in HALVES:
-            to_partner(h, 0, n).start()
-    for n in range(count):
-        for h in HALVES:
-            arrived(h, near[h], n, f_recv.at[h, n])
-            second_hop(h, 1, n).start()
-            to_partner(h, 1, n).start()
-        for h in HALVES:
-            arrived(h, near[1 - h], n, s_recv.at[h, 0, n])
-            to_partner(h, 2, n).start()
-    for n in range(count):
-        for h in HALVES:
-            arrived(h, far, n, s_recv.at[h, 1, n])
-            to_partner(h, 3, n).start()
-    ps = dev(y, x, 1 - c)
-    pshares = lambda h: (ps, (dev(yn, x, 1 - c), dev(y, xn, 1 - c))[h],
-                         (dev(yn, x, 1 - c), dev(y, xn, 1 - c))[1 - h], dev(yn, xn, 1 - c))
-    for which in range(4):
-        for n in range(count):
-            for h in HALVES:
-                arrived(h, pshares(h)[which], n, p_recv.at[h, which, n])
-                to_partner(h, which, n).wait_send()
-    for n in range(count):
-        for h in HALVES:
-            first_hop(h, n).wait_send()
-            for which in HALVES:
-                second_hop(h, which, n).wait_send()
-
-
-def run_gather(o):
+        copy(h, share, q, count, s_send.at[h, which], s_recv.at[h, which, q], near[1 - h])
+
+    def arrived(h, count, sem):
+        span_ = view(h, 0, 0, count)
+        pltpu.make_async_copy(span_, span_, sem).wait()
+
+    def send_own(q, count):
+        for n in range(2 * count):
+            block_copy(2 * CH * q + n).wait()
+        for h in HALVES:
+            copy(h, me, q, count, f_send.at[h], f_recv.at[h, q], near[h])
+            second_hop(h, 0, q, count)
+        for h in HALVES:
+            to_partner(h, 0, q, count)
+
+    def forward_near(q, count):
+        for h in HALVES:
+            arrived(h, count, f_recv.at[h, q])
+            second_hop(h, 1, q, count)
+            to_partner(h, 1, q, count)
+        for h in HALVES:
+            arrived(h, count, s_recv.at[h, 0, q])
+            to_partner(h, 2, q, count)
+
+    def forward_far(q, count):
+        for h in HALVES:
+            arrived(h, count, s_recv.at[h, 1, q])
+            to_partner(h, 3, q, count)
+
+    one = jnp.ones((8, 128), jnp.float32)
+
+    def power(b):
+        square = b * b
+        cube = b * square
+        return cube * (square * square)
+
+    start_loads(jnp.int32(0))
+    norm = jnp.sqrt(jnp.sum(nrm_ref[...], keepdims=True) * (1.0 / 64.0))
+    clip = jnp.minimum(1.0, (one * max_norm) / (norm + CLIP_EPS))
+    cbuf[0] = clip * 0.125
+    cbuf[1] = one / (one * (1.0 - power(b1)))
+    cbuf[2] = one / (one * (1.0 - power(b2)))
+    g_copy(0, 2).start()
+    g_copy(0, 2).wait()
+    place(gbuf, ROWS, ROWS, lambda: gin[2])
+
+    whole = OWN_HALF // CH
+    step(jnp.int32(0))
+
+    def inner(n, q):
+        i = 2 * CH * q + n + 1
+        step(i)
+        finish(i)
+
+        @pl.when((n == 0) & (q >= 1))
+        def _():
+            send_own(q - 1, CH)
+        return q
+
+    def outer(q, carry):
+        lax.fori_loop(0, 2 * CH, inner, q)
+        pl.when(q >= NEAR_LAG)(lambda: forward_near(q - NEAR_LAG, CH))
+        pl.when(q >= FAR_LAG)(lambda: forward_far(q - FAR_LAG, CH))
+        return carry
+
+    lax.fori_loop(0, whole, outer, 0)
+    send_own(whole - 1, CH)
+
+    def last(i, carry):
+        step(i)
+        finish(i)
+        return carry
+
+    lax.fori_loop(OWN - 1, OWN + 1, last, 0)
+    send_own(whole, 1)
+
+    def rest(fn, first):
+        def body(q, carry):
+            fn(q, CH)
+            return carry
+        lax.fori_loop(first, whole, body, 0)
+    rest(forward_near, whole - NEAR_LAG)
+    forward_near(whole, 1)
+    rest(forward_far, whole - FAR_LAG)
+    forward_far(whole, 1)
+    for i in (OWN - 2, OWN - 1):
+        for n in STATE:
+            store_copy(i, n).wait()
+
+    def from_partner(q, count):
+        for h in HALVES:
+            for which in ALL:
+                arrived(h, count, p_recv.at[h, which, q])
+    rest(from_partner, 0)
+    from_partner(whole, 1)
+    for h in HALVES:
+        arrived(h, OWN_HALF, f_send.at[h])
+        for which in HALVES:
+            arrived(h, OWN_HALF, s_send.at[h, which])
+        for which in ALL:
+            arrived(h, OWN_HALF, p_send.at[h, which])
+
+
+def run_update(hyper, nrm, g, state, tails):
+    f32, bf16, dma = jnp.float32, jnp.bfloat16, pltpu.SemaphoreType.DMA
     any_spec = pl.BlockSpec(memory_space=pl.ANY)
-    dma = pltpu.SemaphoreType.DMA
-    count = len(GATHER_CHUNKS)
+    chunks = OWN_HALF // CH + 1
+    rows = pltpu.VMEM((2 * ROWS + 8, 128), f32)
+    flat = pltpu.VMEM((6 * BLK,), f32)
     return pl.pallas_call(
-        gather_kernel, out_shape=jax.ShapeDtypeStruct(o.shape, o.dtype),
-        in_specs=[any_spec], out_specs=any_spec, input_output_aliases={0: 0},
-        scratch_shapes=[dma((2, count)), dma((2, count)), dma((2, 2, count)), dma((2, 2, count)),
-                        dma((2, 4, count)), dma((2, 4, count))],
+        update_kernel,
+        in_specs=[pl.BlockSpec(memory_space=pltpu.SMEM), pl.BlockSpec(memory_space=pltpu.VMEM)] + [any_spec] * 7,
+        out_specs=[any_spec] * 4,
+        out_shape=[jax.ShapeDtypeStruct((OWN * BLK,), f32)] * 3
+        + [jax.ShapeDtypeStruct((GROUP * OWN_HALF, 2) + TILE, bf16)],
+        scratch_shapes=[
+            rows, rows, pltpu.VMEM((ROWS, 128), f32), pltpu.VMEM((3, 128, 128), f32),
+            pltpu.VMEM((3, 8, 128), f32), pltpu.VMEM((3, ROWS, 128), f32), flat, flat,
+            pltpu.VMEM((SLOTS,) + TILE, bf16),
+            dma((3, 4)), dma((PAIR, 3)), dma((SLOTS,)), dma((PAIR,)), dma((PAIR, chunks)), dma((PAIR, 2)),
+            dma((PAIR, 2, chunks)), dma((PAIR, 4)), dma((PAIR, 4, chunks))],
         compiler_params=pltpu.CompilerParams(collective_id=1, has_side_effects=True),
-        name="all_gather",
-    )(o)
+        name="update_gather",
+    )(hyper, nrm, g, *state, *tails)
 
 
 def pack(grads):
@@ -737,7 +803,6 @@
         first_part, second_part, master_part, hyper_params = arrays[GRAD_COUNT:]
         state = (first_part, second_part, master_part)
         shapes = [grad_arr.shape[1:] for grad_arr in grads]
-        me = lax.axis_index("dp").astype(jnp.int32).reshape(1)
 
         heads = jnp.concatenate([s[:BLK] for s in state])
         heads = lax.ppermute(heads, "dp", [(r + 1, r) for r in range(GROUP - 1)])
@@ -746,9 +811,9 @@
                  for n, s in enumerate(state)]
 
         g, nrm = run_reduce(pack(grads))
-        m1, v1, p1, o = run_update(me, hyper_params, nrm, g, state, tails)
-        params = run_unpack(run_gather(o), shapes)
-        return params + (m1, v1, p1)
+        *moved, o = run_update(hyper_params, nrm, g, state, tails)
+        params = run_unpack(o.reshape((-1,) + TILE), shapes)
+        return params + tuple(a[:SHARE] for a in moved)
 
     in_specs = tuple([P("dp")] * GRAD_COUNT + [P("dp"), P("dp"), P("dp"), P()])
     out_specs = tuple([P()] * GRAD_COUNT + [P("dp"), P("dp"), P("dp")])

time: 1160 us -> 1030 us (0.89)
  Pallas kernels: 1130 us -> 956 us
  local copies, waits for them, and re-layouts: 22.4 us -> 58.2 us
    pallas_call x2 -> x1, Pallas kernels: 476 us -> 305 us  [run_update(): pl.pallas_call(update_kernel, in_specs=[pl.BlockSpec(memory_space=pltpu.S...]
    slice x0 -> x3, local copies, waits for them, and re-layouts: none -> 31.4 us  [local_update(): return params + tuple((a[:SHARE] for a in moved))]
where the time goes in v2:
time: 1030 us; the launch traced here: 1020 us
  Pallas kernels  956 us (93%)
  local copies, waits for them, and re-layouts  58.2 us (6%)
    pallas_call x1, Pallas kernels, run_reduce(): pl.pallas_call(reduce_kernel, out_shape=out_shape, in_specs=[any_spec] *...  605 us
    pallas_call x1, Pallas kernels, run_update(): pl.pallas_call(update_kernel, in_specs=[pl.BlockSpec(memory_space=pltpu.S...  305 us
    pallas_call x1, Pallas kernels, run_unpack(): pl.pallas_call(unpack_kernel, out_shape=[jax.ShapeDtypeStruct(s, bf16) fo...  46.8 us
    slice x3, local copies, waits for them, and re-layouts, local_update(): return params + tuple((a[:SHARE] for a in moved))  31.4 us
  transfers between devices with their start and end apart: 1, of which 0 were waited for; matrix products, arithmetic and copies ran while one was open for 1% of the time, Pallas kernels for 0%

profile of v2, /device:TPU:0, one launch (start us, length us, event | category | flops | bytes accessed | tf_op | source)
XLA Modules:
  0.0 1020.9 jit_solution(10972889721845405372)
XLA Ops:
  0.6 0.9 slice.47
  1.6 0.9 slice.48
  2.5 0.9 slice.49
  3.5 1.3 collective-permute-start
  5.5 1.0 reshape_squeeze.18
  6.6 0.8 copy.34
  7.4 1.2 copy.28
  8.7 1.2 copy.29
  9.9 1.7 copy.27
  11.6 4.3 pad_maximum_fusion.q_in
  15.8 604.8 %reduce_scatter.1 = (f32[35712,128]{1,0:T(8,128)}, f32[8,128]{1,0:T(8,128)}, bf16[2,3,2,62,36,8,128]{6,5,4,3,2,1,0:T(8,128)(2,1)}, f32[2,62,36,8,128]{4,3,2,1,0:T(8,128)}) custom-call(bf16[250,36,8,128]{3,2,1,0:T(8,128)(2,1)} %bitcast.98, bf16[72,36,8,128]{3,2,1,0:T(8,128)(2,1)} %pad_maximum_fusion.q_in, bf16[6,36,36,8,128]{4,3,2,1,0:T(8,128)(2,1)} %bitcast.101, ...), custom_call_target="tpu_custom_call" | custom-call | tf_op jit(solution)/shard_map/reduce_scatter/pallas_call | solution.py:377
  620.8 3.2 concatenate.23.pt
  623.9 3.1 concatenate.22.vt
  627.1 3.1 concatenate.21.mt
  630.2 304.6 %update_gather.1 = (f32[4497408]{0:T(1024)}, f32[4497408]{0:T(1024)}, f32[4497408]{0:T(1024)}, bf16[488,2,36,8,128]{4,3,2,1,0:T(8,128)(2,1)}) custom-call(f32[5]{0:T(128)} %hyper_ref.1, f32[8,128]{1,0:T(8,128)} %get-tuple-element.28.nrm_ref, f32[35712,128]{1,0:T(8,128)} %get-tuple-element.29.g_hbm, f32[4483776]{0:T(1024)} %m_hbm.1, f32[4483776]{0:T(1024)} %v_hbm.1, ...), custom_call_target="tpu_custom_call" | custom-call | tf_op jit(solution)/shard_map/update_gather/pallas_call | solution.py:642
  934.8 46.8 %unpack.1 = (bf16[250,36,8,128]{3,2,1,0:T(8,128)(2,1)}, bf16[6,4,36,8,128]{4,3,2,1,0:T(8,128)(2,1)}, bf16[6,2,36,8,128]{4,3,2,1,0:T(8,128)(2,1)}, bf16[6,2,36,8,...) custom-call(bf16[976,36,8,128]{3,2,1,0:T(8,128)(2,1)} %bitcast.36.o), custom_call_target="tpu_custom_call" | custom-call | tf_op jit(solution)/shard_map/unpack/pallas_call | solution.py:776
  981.6 1.0 slice.64
  982.6 1.0 copy.32
  983.7 0.8 reshape.115
  985.1 15.9 %slice.58 = f32[4483776]{0:T(1024)} slice(f32[4497408]{0:T(1024)} %get-tuple-element.40), slice={[0:4483776]} | slice | bytes 35870208 | tf_op jit(solution)/shard_map/slice | solution.py:816
  1001.0 1.8 copy-done
  1002.8 9.0 slice.59
  1012.0 2.0 slice-done.6
  1014.3 6.6 slice.60
  (27 shorter events, 2.1 us)
Async XLA Ops:
  3.5 617.2 %collective-permute-start = (f32[110592]{0:T(1024)S(1)}, f32[110592]{0:T(1024)S(1)}, u32[]{:S(2)}, u32[]{:S(2)}) collective-permute-start(f32[110592]{0:T(1024)S(1)} %pad_maximum_fusion.1), channel_id=1, source_target_pairs={{1,0},{2,1},{3,2},{4,3},{5,4},{6,5},{7,6}} | collective-permute-start | bytes 1327112 | tf_op jit(solution)/shard_map/ppermute | solution.py:808
  15.8 604.9 %slice-start.2 = ((f32[4483776]{0:T(1024)}), f32[23232]{0:T(1024)S(1)}, s32[]{:S(2)}) async-start(f32[4483776]{0:T(1024)} %p_hbm.1), calls=%async_computation.2 | async-start | bytes 188416 | tf_op jit(solution)/shard_map/slice | solution.py:810
  15.8 608.1 %slice-start.1 = ((f32[4483776]{0:T(1024)}), f32[23232]{0:T(1024)S(1)}, s32[]{:S(2)}) async-start(f32[4483776]{0:T(1024)} %v_hbm.1), calls=%async_computation.1 | async-start | bytes 188416 | tf_op jit(solution)/shard_map/slice | solution.py:810
  15.8 611.2 %slice-start = ((f32[4483776]{0:T(1024)}), f32[23232]{0:T(1024)S(1)}, s32[]{:S(2)}) async-start(f32[4483776]{0:T(1024)} %m_hbm.1), calls=%async_computation | async-start | bytes 188416 | tf_op jit(solution)/shard_map/slice | solution.py:810
  985.1 17.8 %copy-start = (f32[4497408]{0:T(1024)S(1)}, f32[4497408]{0:T(1024)}, u32[]{:S(2)}) copy-start(f32[4497408]{0:T(1024)} %get-tuple-element.41) | copy-start | bytes 53968900
  985.1 26.8 %slice-start.3 = ((s8[17989632]{0:T(1024)(128)(4,1)}), s8[4194304]{0:T(1024)(128)(4,1)S(1)}, s32[]{:S(2)}) async-start(s8[17989632]{0:T(1024)(128)(4,1)} %bitcast.99), calls=%async_computation.3 | async-start | bytes 8388608
  985.1 26.8 %slice-start.4 = ((s8[17989632]{0:T(1024)(128)(4,1)}), s8[4194304]{0:T(1024)(128)(4,1)S(1)}, s32[]{:S(2)}) async-start(s8[17989632]{0:T(1024)(128)(4,1)} %bitcast.99), calls=%async_computation.4 | async-start | bytes 8388608
  985.1 26.9 %slice-start.5 = ((s8[17989632]{0:T(1024)(128)(4,1)}), s8[4194304]{0:T(1024)(128)(4,1)S(1)}, s32[]{:S(2)}) async-start(s8[17989632]{0:T(1024)(128)(4,1)} %bitcast.99), calls=%async_computation.5 | async-start | bytes 8388608
  1002.8 11.2 %slice-start.6 = ((s8[17989632]{0:T(1024)(128)(4,1)}), s8[4194304]{0:T(1024)(128)(4,1)S(1)}, s32[]{:S(2)}) async-start(s8[17989632]{0:T(1024)(128)(4,1)} %bitcast.99), calls=%async_computation.6 | async-start | bytes 8388608
  1002.8 11.5 %slice-start.7 = ((s8[17989632]{0:T(1024)(128)(4,1)}), s8[1212416]{0:T(1024)(128)(4,1)S(1)}, s32[]{:S(2)}) async-start(s8[17989632]{0:T(1024)(128)(4,1)} %bitcast.99), calls=%async_computation.7 | async-start | bytes 2424832

commit v3 on v2

--- a/solution.py
+++ b/solution.py
@@ -31,12 +31,13 @@
 SLOTS = 8
 OWN = 122
 OWN_HALF = OWN // 2
-EDGES = (0, 250, 274, 286, 298, 322, 538, 754, 970, 974)
+EDGES = (0, 250, 274, 286, 298, 322, 538, 754, 970, 976)
 TAIL_BLOCKS = 6
 TILE = (36, 8, 128)
 COLS = 36
 NEAR_LAG = 2
 FAR_LAG = 4
+PART = 2
 DECAY_LEN = 970 * BLK
 
 
@@ -167,26 +168,30 @@
 
 
 def by_block(b, refs, fn):
-    embed, small, gate, up, down, tail = refs
-    e = EDGES
-
-    def span(lo, hi, view):
-        @pl.when((b >= lo) & (b < hi))
-        def _():
-            fn(view(b - lo))
-    span(0, e[1], lambda n: embed.at[n])
-    span(e[1], e[5], lambda n: small.at[n])
-    span(e[5], e[6], lambda n: gate.at[n // COLS, :, n % COLS])
-    span(e[6], e[7], lambda n: up.at[n // COLS, :, n % COLS])
-    span(e[7], e[8], lambda n: down.at[n])
-    span(e[8], e[8] + TAIL_BLOCKS, lambda n: tail.at[n])
-
-
-def reduce_kernel(e_in, q_in, gate_in, up_in, down_in, tail_in, g_hbm, nrm_ref, r1, r2, ld, ld2, st, sbuf, tbuf, fbuf, acc, nbuf,
+    for kind, ref in enumerate(refs):
+        first, last = EDGES[kind], EDGES[kind + 1]
+        shape = ref.shape
+
+        @pl.when((b >= first) & (b < last))
+        def _(ref=ref, shape=shape, n=b - first):
+            if len(shape) == 4:
+                fn(ref.at[n], 0, COLS)
+                return
+            high = shape[1]
+            wide = COLS // high
+            layer, part = n // high, n % high
+            if wide == 1:
+                fn(ref.at[layer, :, part], 0, COLS)
+            else:
+                for rt in range(high):
+                    fn(ref.at[layer, rt, pl.ds(part * wide, wide)], rt * wide, wide)
+
+
+def reduce_kernel(e_in, q_in, k_in, v_in, o_in, gate_in, up_in, down_in, tail_in, g_hbm, nrm_ref, r1, r2, ld, ld2, st, sbuf, tbuf, fbuf, acc, nbuf,
                   s1_send, s1_recv, s2_send, s2_recv, ld_sem, g_sem, n_send, n_recv):
     me = lax.axis_index("dp")
     y, x, c, xn, yn = positions(me)
-    sources = (e_in, q_in, gate_in, up_in, down_in, tail_in)
+    sources = (e_in, q_in, k_in, v_in, o_in, gate_in, up_in, down_in, tail_in)
     barrier = pltpu.get_barrier_semaphore()
     for o in OTHERS:
         pl.semaphore_signal(barrier, inc=1, device_id=((me + o) % GROUP,), device_id_type=MESH)
@@ -210,9 +215,9 @@
         for j in range(CH):
             at = k * CH + j
 
-            def start(src):
+            def start(src, tile, tiles):
                 pltpu.make_async_remote_copy(
-                    src_ref=src, dst_ref=r1.at[h, slot, d, at],
+                    src_ref=src, dst_ref=r1.at[h, slot, d, at, pl.ds(tile, tiles)],
                     send_sem=s1_send.at[h, n, t % SLOTS], recv_sem=s1_recv.at[h, slot, t],
                     device_id=(device,), device_id_type=MESH).start()
             by_block(cover_start(dest) + h * HALF + at, sources, start)
@@ -250,8 +255,9 @@
     def start_loads(h, t, dest):
         d, k = t // CHUNKS, t % CHUNKS
         for j in range(CH):
-            def start(src):
-                pltpu.make_async_copy(src, ld.at[h, 3, j], ld_sem.at[h, 3]).start()
+            def start(src, tile, tiles):
+                pltpu.make_async_copy(
+                    src, ld.at[h, 3, j, pl.ds(tile, tiles)], ld_sem.at[h, 3]).start()
             by_block(cover_start(dest) + h * HALF + k * CH + j, sources, start)
         for slot in range(3):
             pltpu.make_async_copy(
@@ -413,7 +419,7 @@
     rho, odd = delta // 128, me % 2 == 1
     sigma = (own_start(me) * BLK - me * SHARE) // 128
     low, high = pl.ds(0, ROWS), pl.ds(ROWS, ROWS)
-    state, tails, outs = (m_hbm, v_hbm, p_hbm), (mt, vt, pt), (m_out, v_out, p_out)
+    state, tails, outs = (m_hbm, v_hbm, p_hbm), (mt, vt, pt), (m_out, v_out)
     size = 32
     lane = lax.broadcasted_iota(jnp.int32, (size, 128), 1)
     sub = lax.broadcasted_iota(jnp.int32, (size, 128), 0)
@@ -454,8 +460,9 @@
                 pltpu.make_async_copy(
                     tails[n].at[span(i - OWN + 1)], sin.at[flat(i, n)], in_sem.at[i % 2, n]).start()
 
-    def store_copy(i, n):
-        return pltpu.make_async_copy(sout.at[flat(i, n)], outs[n].at[span(i)], out_sem.at[i % 2, n])
+    def store_copy(i):
+        return pltpu.make_async_copy(
+            sout.at[pl.ds(pl.multiple_of(i % 2 * BLK, 1024), BLK)], p_out.at[span(i)], out_sem.at[i % 2])
 
     def block_copy(j):
         return pltpu.make_async_copy(
@@ -469,15 +476,11 @@
         for n in STATE:
             view = sin.at[flat(i, n)]
             pltpu.make_async_copy(view, view, in_sem.at[i % 2, n]).wait()
-
-            @pl.when((i >= 2) & (i < OWN))
-            def _():
-                store_copy(i - 2, n).wait()
+        pl.when(i >= 2)(lambda: store_copy(i - 2).wait())
         gbuf[low, :] = gbuf[high, :]
         pbuf[low, :] = pbuf[high, :]
         place(gbuf, ROWS, ROWS, lambda: gin[i % 2])
         scale, inv1, inv2 = [cbuf[n, :1] for n in STATE]
-        keep = i < OWN
         for j in range(ROWS // size):
             first, count = size * 128 * j, size * 128
             h = window(gbuf, rho, j) * scale
@@ -489,16 +492,14 @@
             u = (m1 * inv1) / (jnp.sqrt(v1 * inv2) + ADAM_EPS) + decay
             p1 = p - lr * u
             place(pbuf, ROWS + size * j, size, lambda: p1)
-
-            @pl.when(keep)
+            sout[pl.ds(pl.multiple_of(i % 2 * BLK + first, 1024), count)] = p1.reshape(count)
+
+            @pl.when(i < OWN)
             def _():
-                for n, value in enumerate((m1, v1, p1)):
-                    sout[flat(i, n, first, count)] = value.reshape(count)
-
-        @pl.when(keep)
-        def _():
-            for n in STATE:
-                store_copy(i, n).start()
+                for n, value in enumerate((m1, v1)):
+                    outs[n][pl.ds(pl.multiple_of(i * BLK + first, 1024), count)] = value.reshape(count)
+
+        pl.when(i < OWN)(lambda: store_copy(i).start())
 
     def finish(i):
         j = i - 1
@@ -516,7 +517,7 @@
         block_copy(j).start()
 
     def view(h, share, q, count):
-        return o.at[pl.ds(share * OWN_HALF + q * CH, count), h]
+        return o.at[pl.ds(share * OWN_HALF + q * PART, count), h]
 
     def copy(h, share, q, count, send, recv, device):
         span_ = view(h, share, q, count)
@@ -538,7 +539,7 @@
 
     def send_own(q, count):
         for n in range(2 * count):
-            block_copy(2 * CH * q + n).wait()
+            block_copy(2 * PART * q + n).wait()
         for h in HALVES:
             copy(h, me, q, count, f_send.at[h], f_recv.at[h, q], near[h])
             second_hop(h, 0, q, count)
@@ -576,27 +577,27 @@
     g_copy(0, 2).wait()
     place(gbuf, ROWS, ROWS, lambda: gin[2])
 
-    whole = OWN_HALF // CH
+    whole = (OWN_HALF - 1) // PART
     step(jnp.int32(0))
 
     def inner(n, q):
-        i = 2 * CH * q + n + 1
+        i = 2 * PART * q + n + 1
         step(i)
         finish(i)
 
         @pl.when((n == 0) & (q >= 1))
         def _():
-            send_own(q - 1, CH)
+            send_own(q - 1, PART)
         return q
 
     def outer(q, carry):
-        lax.fori_loop(0, 2 * CH, inner, q)
-        pl.when(q >= NEAR_LAG)(lambda: forward_near(q - NEAR_LAG, CH))
-        pl.when(q >= FAR_LAG)(lambda: forward_far(q - FAR_LAG, CH))
+        lax.fori_loop(0, 2 * PART, inner, q)
+        pl.when(q >= NEAR_LAG)(lambda: forward_near(q - NEAR_LAG, PART))
+        pl.when(q >= FAR_LAG)(lambda: forward_far(q - FAR_LAG, PART))
         return carry
 
     lax.fori_loop(0, whole, outer, 0)
-    send_own(whole - 1, CH)
+    send_own(whole - 1, PART)
 
     def last(i, carry):
         step(i)
@@ -608,16 +609,15 @@
 
     def rest(fn, first):
         def body(q, carry):
-            fn(q, CH)
+            fn(q, PART)
             return carry
         lax.fori_loop(first, whole, body, 0)
     rest(forward_near, whole - NEAR_LAG)
     forward_near(whole, 1)
     rest(forward_far, whole - FAR_LAG)
     forward_far(whole, 1)
-    for i in (OWN - 2, OWN - 1):
-        for n in STATE:
-            store_copy(i, n).wait()
+
+    store_copy(OWN - 1).wait()
 
     def from_partner(q, count):
         for h in HALVES:
@@ -636,22 +636,22 @@
 def run_update(hyper, nrm, g, state, tails):
     f32, bf16, dma = jnp.float32, jnp.bfloat16, pltpu.SemaphoreType.DMA
     any_spec = pl.BlockSpec(memory_space=pl.ANY)
-    chunks = OWN_HALF // CH + 1
+    chunks = (OWN_HALF - 1) // PART + 1
     rows = pltpu.VMEM((2 * ROWS + 8, 128), f32)
     flat = pltpu.VMEM((6 * BLK,), f32)
     return pl.pallas_call(
         update_kernel,
         in_specs=[pl.BlockSpec(memory_space=pltpu.SMEM), pl.BlockSpec(memory_space=pltpu.VMEM)] + [any_spec] * 7,
-        out_specs=[any_spec] * 4,
-        out_shape=[jax.ShapeDtypeStruct((OWN * BLK,), f32)] * 3
+        out_specs=[pl.BlockSpec(memory_space=pltpu.VMEM)] * PAIR + [any_spec] * PAIR,
+        out_shape=[pltpu.VMEM((OWN * BLK,), f32)] * PAIR + [jax.ShapeDtypeStruct((OWN * BLK,), f32)]
         + [jax.ShapeDtypeStruct((GROUP * OWN_HALF, 2) + TILE, bf16)],
         scratch_shapes=[
             rows, rows, pltpu.VMEM((ROWS, 128), f32), pltpu.VMEM((3, 128, 128), f32),
-            pltpu.VMEM((3, 8, 128), f32), pltpu.VMEM((3, ROWS, 128), f32), flat, flat,
+            pltpu.VMEM((3, 8, 128), f32), pltpu.VMEM((3, ROWS, 128), f32), flat, pltpu.VMEM((PAIR * BLK,), f32),
             pltpu.VMEM((SLOTS,) + TILE, bf16),
-            dma((3, 4)), dma((PAIR, 3)), dma((SLOTS,)), dma((PAIR,)), dma((PAIR, chunks)), dma((PAIR, 2)),
+            dma((3, 4)), dma((PAIR,)), dma((SLOTS,)), dma((PAIR,)), dma((PAIR, chunks)), dma((PAIR, 2)),
             dma((PAIR, 2, chunks)), dma((PAIR, 4)), dma((PAIR, 4, chunks))],
-        compiler_params=pltpu.CompilerParams(collective_id=1, has_side_effects=True),
+        compiler_params=pltpu.CompilerParams(collective_id=1, has_side_effects=True, vmem_limit_bytes=6 * 2**20),
         name="update_gather",
     )(hyper, nrm, g, *state, *tails)
 
@@ -666,15 +666,9 @@
         layers, wide, high = a.shape
         return a.transpose(0, 2, 1).reshape(layers, high // 8, 8, COLS, 128).transpose(0, 1, 3, 2, 4)
 
-    def cols(a, parts):
-        a = grid(a)
-        a = a.reshape(a.shape[0], a.shape[1], parts, -1, 8, 128).swapaxes(1, 2)
-        return a.reshape((-1,) + TILE)
-
     tail = jnp.concatenate([norms.reshape(-1), qk.reshape(-1)])
     tail = jnp.pad(tail, (0, TAIL_BLOCKS * BLK - tail.shape[0]))
-    small = jnp.concatenate([cols(q, 4), cols(k, 2), cols(v, 2), rows(out)])
-    return rows(embed), small, grid(gate), grid(up), rows(down), rows(tail.reshape(-1, 4608))
+    return rows(embed), grid(q), grid(k), grid(v), rows(out), grid(gate), grid(up), rows(down), rows(tail.reshape(-1, 4608))
 
 
 def block_runs(b0, b1):
@@ -723,7 +717,7 @@
             jobs.append((lo, hi - lo, rows_out(ref, lo - b0)))
 
     e = EDGES
-    add_rows(embed, e[0], e[1])
+    add_rows(embed, 0, e[1])
     for layer in range(gate.shape[0]):
         jobs.append((e[5] + COLS * layer, COLS, grid_out(gate, layer)))
         jobs.append((e[6] + COLS * layer, COLS, grid_out(up, layer)))
@@ -732,7 +726,7 @@
     jobs.append((e[3], e[4] - e[3], cols_out(v, 2)))
     add_rows(out, e[4], e[5])
     add_rows(down, e[7], e[8])
-    add_rows(tail, e[8], e[9])
+    add_rows(tail, e[8], e[8] + 4)
     depth = buf.shape[0]
 
     def load(n):
@@ -770,13 +764,14 @@
     def grid(shape):
         return (shape[0], shape[2] // 8) + TILE
     views = [rows(e[1]), grid(shapes[1]), grid(shapes[2]), grid(shapes[3]), rows(e[5] - e[4]),
-             grid(shapes[5]), grid(shapes[6]), rows(e[8] - e[7]), rows(e[9] - e[8])]
+             grid(shapes[5]), grid(shapes[6]), rows(e[8] - e[7]), rows(4)]
     dma = pltpu.SemaphoreType.DMA
-    depth = 6
+    depth = 4
     outs = pl.pallas_call(
         unpack_kernel, out_shape=[jax.ShapeDtypeStruct(s, bf16) for s in views],
         in_specs=[any_spec], out_specs=[any_spec] * len(views),
         scratch_shapes=[pltpu.VMEM((depth, COLS) + TILE, bf16), dma((depth,)), dma((depth,))],
+        compiler_params=pltpu.CompilerParams(vmem_limit_bytes=12 * 2**20),
         name="unpack",
     )(o)
 
@@ -812,8 +807,8 @@
 
         g, nrm = run_reduce(pack(grads))
         *moved, o = run_update(hyper_params, nrm, g, state, tails)
-        params = run_unpack(o.reshape((-1,) + TILE), shapes)
-        return params + tuple(a[:SHARE] for a in moved)
+        o, *moved = lax.optimization_barrier([o] + [a[:SHARE] for a in moved])
+        return run_unpack(o.reshape((-1,) + TILE), shapes) + tuple(moved)
 
     in_specs = tuple([P("dp")] * GRAD_COUNT + [P("dp"), P("dp"), P("dp"), P()])
     out_specs = tuple([P()] * GRAD_COUNT + [P("dp"), P("dp"), P("dp")])

time: 1030 us -> 1000 us (0.971)
  local copies, waits for them, and re-layouts: 58.2 us -> 37.2 us
  transfers between devices with their start and end apart: 1 -> 1, of which waited for: 0 -> 0; matrix products, arithmetic and copies ran while one was open for 1% -> 0% of each run, Pallas kernels for 0% -> 0%
where the time goes in v3:
time: 1000 us; the launch traced here: 996 us
  Pallas kernels  957 us (96%)
  local copies, waits for them, and re-layouts  37.2 us (4%)
    pallas_call x1, Pallas kernels, run_reduce(): pl.pallas_call(reduce_kernel, out_shape=out_shape, in_specs=[any_spec] *...  606 us
    pallas_call x1, Pallas kernels, run_update(): pl.pallas_call(update_kernel, in_specs=[pl.BlockSpec(memory_space=pltpu.S...  304 us
    pallas_call x1, Pallas kernels, run_unpack(): pl.pallas_call(unpack_kernel, out_shape=[jax.ShapeDtypeStruct(s, bf16) fo...  46.6 us
    slice x3, local copies, waits for them, and re-layouts, local_update(): o, *moved = lax.optimization_barrier([o] + [a[:SHARE] for a in moved])  22.1 us
  transfers between devices with their start and end apart: 1, of which 0 were waited for; matrix products, arithmetic and copies ran while one was open for 0% of the time, Pallas kernels for 0%

profile of v3, /device:TPU:0, one launch (start us, length us, event | category | flops | bytes accessed | tf_op | source)
XLA Modules:
  0.0 996.3 jit_solution(894483045195087081)
XLA Ops:
  0.6 0.9 slice.47
  1.6 0.9 slice.48
  2.5 0.9 slice.49
  3.5 1.3 collective-permute-start
  4.8 0.7 reshape_squeeze.19
  5.5 1.0 reshape_squeeze.18
  6.5 0.1 reshape_reshape.3
  6.6 0.8 copy.31
  7.4 605.8 %reduce_scatter.1 = (f32[35712,128]{1,0:T(8,128)}, f32[8,128]{1,0:T(8,128)}, bf16[2,3,2,62,36,8,128]{6,5,4,3,2,1,0:T(8,128)(2,1)}, f32[2,62,36,8,128]{4,3,2,1,0:T(8,128)}) custom-call(bf16[250,36,8,128]{3,2,1,0:T(8,128)(2,1)} %bitcast.85, bf16[6,4,36,8,128]{4,3,2,1,0:T(8,128)(2,1)} %bitcast.90, bf16[6,2,36,8,128]{4,3,2,1,0:T(8,128)(2,1)} %bitcast.92, ...), custom_call_target="tpu_custom_call" | custom-call | tf_op jit(solution)/shard_map/reduce_scatter/pallas_call | solution.py:383
  613.3 0.0 collective-permute-done
  613.4 1.4 concatenate.19.pt
  614.7 1.4 concatenate.18.vt
  616.1 1.4 concatenate.17.mt
  617.5 0.7 copy-done
  618.2 304.4 %update_gather.1 = (f32[4497408]{0:T(1024)S(1)}, f32[4497408]{0:T(1024)S(1)}, f32[4497408]{0:T(1024)}, bf16[488,2,36,8,128]{4,3,2,1,0:T(8,128)(2,1)}) custom-call(f32[5]{0:T(128)S(1)} %copy-done.1, f32[8,128]{1,0:T(8,128)S(1)} %copy-done, f32[35712,128]{1,0:T(8,128)} %get-tuple-element.33.g_hbm, f32[4483776]{0:T(1024)} %m_hbm.1, f32[4483776]{0:T(1024)} %v_hbm.1, ...), custom_call_target="tpu_custom_call" | custom-call | tf_op jit(solution)/shard_map/update_gather/pallas_call | solution.py:642
  922.6 6.6 slice.55
  929.2 9.0 slice.56
  938.2 3.3 copy-done.2
  941.5 6.6 slice.57
  948.1 46.6 %unpack.1 = (bf16[250,36,8,128]{3,2,1,0:T(8,128)(2,1)}, bf16[6,4,36,8,128]{4,3,2,1,0:T(8,128)(2,1)}, bf16[6,2,36,8,128]{4,3,2,1,0:T(8,128)(2,1)}, bf16[6,2,36,8,...) custom-call(bf16[976,36,8,128]{3,2,1,0:T(8,128)(2,1)} %bitcast.27.o), custom_call_target="tpu_custom_call" | custom-call | tf_op jit(solution)/shard_map/unpack/pallas_call | solution.py:770
  994.7 0.1 copy.29
  994.9 0.8 reshape.91
  995.6 0.1 slice.59
  995.7 0.6 slice.65
  (16 shorter events, 0.2 us)
Async XLA Ops:
  3.5 609.8 %collective-permute-start = (f32[110592]{0:T(1024)S(1)}, f32[110592]{0:T(1024)S(1)}, u32[]{:S(2)}, u32[]{:S(2)}) collective-permute-start(f32[110592]{0:T(1024)S(1)} %pad_maximum_fusion), channel_id=1, source_target_pairs={{1,0},{2,1},{3,2},{4,3},{5,4},{6,5},{7,6}} | collective-permute-start | bytes 1327112 | tf_op jit(solution)/shard_map/ppermute | solution.py:803
  7.4 605.9 %slice-start.2 = ((f32[4483776]{0:T(1024)}), f32[23232]{0:T(1024)S(1)}, s32[]{:S(2)}) async-start(f32[4483776]{0:T(1024)} %p_hbm.1), calls=%async_computation.2 | async-start | bytes 188416 | tf_op jit(solution)/shard_map/slice | solution.py:805
  7.4 607.3 %slice-start.1 = ((f32[4483776]{0:T(1024)}), f32[23232]{0:T(1024)S(1)}, s32[]{:S(2)}) async-start(f32[4483776]{0:T(1024)} %v_hbm.1), calls=%async_computation.1 | async-start | bytes 188416 | tf_op jit(solution)/shard_map/slice | solution.py:805
  7.4 608.7 %slice-start = ((f32[4483776]{0:T(1024)}), f32[23232]{0:T(1024)S(1)}, s32[]{:S(2)}) async-start(f32[4483776]{0:T(1024)} %m_hbm.1), calls=%async_computation | async-start | bytes 188416 | tf_op jit(solution)/shard_map/slice | solution.py:805
  7.4 610.1 %copy-start.1 = (f32[5]{0:T(128)S(1)}, f32[5]{0:T(128)}, u32[]{:S(2)}) copy-start(f32[5]{0:T(128)} %hyper_ref.1) | copy-start | bytes 64
  617.5 0.7 copy-start
  929.2 12.3 %copy-start.2 = (f32[4497408]{0:T(1024)S(1)}, f32[4497408]{0:T(1024)}, u32[]{:S(2)}) copy-start(f32[4497408]{0:T(1024)} %get-tuple-element.37) | copy-start | bytes 53968900

commit v4 on v3

--- a/solution.py
+++ b/solution.py
@@ -31,6 +31,8 @@
 SLOTS = 8
 OWN = 122
 OWN_HALF = OWN // 2
+GATHERED = 52
+LATE = OWN - 2 * GATHERED
 EDGES = (0, 250, 274, 286, 298, 322, 538, 754, 970, 976)
 TAIL_BLOCKS = 6
 TILE = (36, 8, 128)
@@ -402,7 +404,7 @@
 
 
 def update_kernel(hyper_ref, nrm_ref, g_hbm, m_hbm, v_hbm, p_hbm, mt, vt, pt,
-                  m_out, v_out, p_out, o, gbuf, pbuf, fbuf, tbuf, cbuf, gin, sin, sout, obuf,
+                  m_out, v_out, p_out, o, late, gbuf, pbuf, fbuf, tbuf, cbuf, gin, sin, sout, obuf,
                   in_sem, out_sem, o_sem, f_send, f_recv, s_send, s_recv, p_send, p_recv):
     me = lax.axis_index("dp")
     y, x, c, xn, yn = positions(me)
@@ -464,9 +466,18 @@
         return pltpu.make_async_copy(
             sout.at[pl.ds(pl.multiple_of(i % 2 * BLK, 1024), BLK)], p_out.at[span(i)], out_sem.at[i % 2])
 
-    def block_copy(j):
-        return pltpu.make_async_copy(
-            obuf.at[j % SLOTS], o.at[me * OWN_HALF + j // 2, j % 2], o_sem.at[j % SLOTS])
+    def block_start(j):
+        @pl.when(j < 2 * GATHERED)
+        def _():
+            pltpu.make_async_copy(
+                obuf.at[j % SLOTS], o.at[me * GATHERED + j // 2, j % 2], o_sem.at[j % SLOTS]).start()
+
+        @pl.when(j >= 2 * GATHERED)
+        def _():
+            pltpu.make_async_copy(obuf.at[j % SLOTS], late.at[j - 2 * GATHERED], o_sem.at[j % SLOTS]).start()
+
+    def block_wait(j):
+        pltpu.make_async_copy(obuf.at[j % SLOTS], late.at[0], o_sem.at[j % SLOTS]).wait()
 
     def step(i):
         @pl.when(i < OWN)
@@ -514,10 +525,10 @@
         pl.when(is_gate)(functools.partial(joined_to_transposed, "gate", fbuf, tbuf, emit))
         pl.when(is_q)(functools.partial(joined_to_transposed, "q", fbuf, tbuf, emit))
         pl.when(is_kv)(functools.partial(joined_to_transposed, "kv", fbuf, tbuf, emit))
-        block_copy(j).start()
+        block_start(j)
 
     def view(h, share, q, count):
-        return o.at[pl.ds(share * OWN_HALF + q * PART, count), h]
+        return o.at[pl.ds(share * GATHERED + q * PART, count), h]
 
     def copy(h, share, q, count, send, recv, device):
         span_ = view(h, share, q, count)
@@ -537,9 +548,11 @@
         span_ = view(h, 0, 0, count)
         pltpu.make_async_copy(span_, span_, sem).wait()
 
+    def stored(q, count):
+        for n in range(2 * count):
+            block_wait(2 * PART * q + n)
+
     def send_own(q, count):
-        for n in range(2 * count):
-            block_copy(2 * PART * q + n).wait()
         for h in HALVES:
             copy(h, me, q, count, f_send.at[h], f_recv.at[h, q], near[h])
             second_hop(h, 0, q, count)
@@ -578,6 +591,7 @@
     place(gbuf, ROWS, ROWS, lambda: gin[2])
 
     whole = (OWN_HALF - 1) // PART
+    handed = GATHERED // PART
     step(jnp.int32(0))
 
     def inner(n, q):
@@ -587,17 +601,18 @@
 
         @pl.when((n == 0) & (q >= 1))
         def _():
-            send_own(q - 1, PART)
+            stored(q - 1, PART)
+            pl.when(q <= handed)(lambda: send_own(q - 1, PART))
         return q
 
     def outer(q, carry):
         lax.fori_loop(0, 2 * PART, inner, q)
-        pl.when(q >= NEAR_LAG)(lambda: forward_near(q - NEAR_LAG, PART))
-        pl.when(q >= FAR_LAG)(lambda: forward_far(q - FAR_LAG, PART))
+        pl.when((q >= NEAR_LAG) & (q - NEAR_LAG < handed))(lambda: forward_near(q - NEAR_LAG, PART))
+        pl.when((q >= FAR_LAG) & (q - FAR_LAG < handed))(lambda: forward_far(q - FAR_LAG, PART))
         return carry
 
     lax.fori_loop(0, whole, outer, 0)
-    send_own(whole - 1, PART)
+    stored(whole - 1, PART)
 
     def last(i, carry):
         step(i)
@@ -605,17 +620,15 @@
         return carry
 
     lax.fori_loop(OWN - 1, OWN + 1, last, 0)
-    send_own(whole, 1)
+    stored(whole, 1)
 
     def rest(fn, first):
         def body(q, carry):
             fn(q, PART)
             return carry
-        lax.fori_loop(first, whole, body, 0)
+        lax.fori_loop(min(first, handed), handed, body, 0)
     rest(forward_near, whole - NEAR_LAG)
-    forward_near(whole, 1)
     rest(forward_far, whole - FAR_LAG)
-    forward_far(whole, 1)
 
     store_copy(OWN - 1).wait()
 
@@ -624,27 +637,26 @@
             for which in ALL:
                 arrived(h, count, p_recv.at[h, which, q])
     rest(from_partner, 0)
-    from_partner(whole, 1)
     for h in HALVES:
-        arrived(h, OWN_HALF, f_send.at[h])
+        arrived(h, GATHERED, f_send.at[h])
         for which in HALVES:
-            arrived(h, OWN_HALF, s_send.at[h, which])
+            arrived(h, GATHERED, s_send.at[h, which])
         for which in ALL:
-            arrived(h, OWN_HALF, p_send.at[h, which])
+            arrived(h, GATHERED, p_send.at[h, which])
 
 
 def run_update(hyper, nrm, g, state, tails):
     f32, bf16, dma = jnp.float32, jnp.bfloat16, pltpu.SemaphoreType.DMA
     any_spec = pl.BlockSpec(memory_space=pl.ANY)
-    chunks = (OWN_HALF - 1) // PART + 1
+    chunks = GATHERED // PART
     rows = pltpu.VMEM((2 * ROWS + 8, 128), f32)
     flat = pltpu.VMEM((6 * BLK,), f32)
     return pl.pallas_call(
         update_kernel,
         in_specs=[pl.BlockSpec(memory_space=pltpu.SMEM), pl.BlockSpec(memory_space=pltpu.VMEM)] + [any_spec] * 7,
-        out_specs=[pl.BlockSpec(memory_space=pltpu.VMEM)] * PAIR + [any_spec] * PAIR,
+        out_specs=[pl.BlockSpec(memory_space=pltpu.VMEM)] * PAIR + [any_spec] * STATE[-1] + [any_spec],
         out_shape=[pltpu.VMEM((OWN * BLK,), f32)] * PAIR + [jax.ShapeDtypeStruct((OWN * BLK,), f32)]
-        + [jax.ShapeDtypeStruct((GROUP * OWN_HALF, 2) + TILE, bf16)],
+        + [jax.ShapeDtypeStruct(n + TILE, bf16) for n in ((GROUP * GATHERED, 2), (LATE,))],
         scratch_shapes=[
             rows, rows, pltpu.VMEM((ROWS, 128), f32), pltpu.VMEM((3, 128, 128), f32),
             pltpu.VMEM((3, 8, 128), f32), pltpu.VMEM((3, ROWS, 128), f32), flat, pltpu.VMEM((PAIR * BLK,), f32),
@@ -672,16 +684,22 @@
 
 
 def block_runs(b0, b1):
-    cuts = [own_start(r) for r in range(GROUP + 1)]
     out = []
     for r in range(GROUP):
-        lo, hi = max(b0, cuts[r]), min(b1, cuts[r + 1])
+        start = own_start(r)
+        lo, hi = max(b0, start), min(b1, own_start(r + 1), start + 2 * GATHERED)
         if lo < hi:
-            out.append((r * OWN + lo - cuts[r], hi - lo))
+            out.append((r * 2 * GATHERED + lo - start, lo - b0, hi - lo))
     return out
 
 
-def unpack_kernel(o, embed, q, k, v, out, gate, up, down, tail, buf, in_sem, out_sem):
+def is_rows(kind):
+    return kind in (0, 4, 7, 8)
+
+
+def unpack_kernel(kinds, o, *refs):
+    outs, (buf, in_sem, out_sem) = refs[:len(kinds)], refs[len(kinds):]
+
     def rows_out(ref, first):
         def store(slot, count):
             pltpu.make_async_copy(
@@ -696,85 +714,143 @@
             lax.fori_loop(0, COLS, one, 0)
         return store
 
-    def cols_out(ref, parts):
-        high, wide = ref.shape[1], COLS // parts
+    def cols_out(ref):
+        high = ref.shape[1]
+        wide = COLS // high
 
         def store(slot, count):
             def one(n, z):
                 for rt in range(high):
                     pltpu.make_async_copy(
                         buf.at[slot, n, pl.ds(wide * rt, wide)],
-                        ref.at[n // parts, rt, pl.ds((n % parts) * wide, wide)], out_sem.at[slot]).start()
+                        ref.at[n // high, rt, pl.ds((n % high) * wide, wide)], out_sem.at[slot]).start()
                 return z
             lax.fori_loop(0, count, one, 0)
         return store
 
     jobs = []
-
-    def add_rows(ref, b0, b1):
-        for lo in range(b0, b1, COLS):
-            hi = min(lo + COLS, b1)
-            jobs.append((lo, hi - lo, rows_out(ref, lo - b0)))
-
-    e = EDGES
-    add_rows(embed, 0, e[1])
-    for layer in range(gate.shape[0]):
-        jobs.append((e[5] + COLS * layer, COLS, grid_out(gate, layer)))
-        jobs.append((e[6] + COLS * layer, COLS, grid_out(up, layer)))
-    jobs.append((e[1], e[2] - e[1], cols_out(q, 4)))
-    jobs.append((e[2], e[3] - e[2], cols_out(k, 2)))
-    jobs.append((e[3], e[4] - e[3], cols_out(v, 2)))
-    add_rows(out, e[4], e[5])
-    add_rows(down, e[7], e[8])
-    add_rows(tail, e[8], e[8] + 4)
+    for kind, ref in zip(kinds, outs):
+        first = EDGES[kind]
+        if is_rows(kind):
+            count = ref.shape[0]
+            for lo in range(0, count, COLS):
+                jobs.append((first + lo, min(COLS, count - lo), rows_out(ref, lo)))
+        elif ref.shape[1] == COLS:
+            for layer in range(ref.shape[0]):
+                jobs.append((first + COLS * layer, COLS, grid_out(ref, layer)))
+        else:
+            jobs.append((first, EDGES[kind + 1] - first, cols_out(ref)))
     depth = buf.shape[0]
 
     def load(n):
         b0, count, _ = jobs[n]
-        at = 0
-        for first, size in block_runs(b0, b0 + count):
+        for first, at, size in block_runs(b0, b0 + count):
             pltpu.make_async_copy(
                 o.at[pl.ds(first, size)], buf.at[n % depth, pl.ds(at, size)], in_sem.at[n % depth]).start()
-            at += size
-
-    def wait(n, sem):
-        view = buf.at[n % depth, pl.ds(0, jobs[n][1])]
-        pltpu.make_async_copy(view, view, sem.at[n % depth]).wait()
+
+    def wait(n, count, sem):
+        if count:
+            view = buf.at[n % depth, pl.ds(0, count)]
+            pltpu.make_async_copy(view, view, sem.at[n % depth]).wait()
+
+    def loaded(n):
+        b0, count, _ = jobs[n]
+        return sum(size for _, _, size in block_runs(b0, b0 + count))
 
     lead = depth // 2
     for n in range(len(jobs) + lead):
         if n < len(jobs):
             if n >= depth:
-                wait(n - depth, out_sem)
+                wait(n - depth, jobs[n - depth][1], out_sem)
             load(n)
         if n >= lead:
-            wait(n - lead, in_sem)
+            wait(n - lead, loaded(n - lead), in_sem)
             jobs[n - lead][2]((n - lead) % depth, jobs[n - lead][1])
     for n in range(len(jobs) - depth, len(jobs)):
-        wait(n, out_sem)
-
-
-def run_unpack(o, shapes):
-    e, bf16 = EDGES, jnp.bfloat16
+        wait(n, jobs[n][1], out_sem)
+
+
+def late_kernel(*refs):
+    count = len(EDGES) - 1
+    late, outs = refs[:GROUP], refs[GROUP + count:GROUP + 2 * count]
+    buf, in_sem, out_sem = refs[GROUP + 2 * count:]
+    me = lax.axis_index("dp")
+    y, x, c, _, _ = positions(me)
+    for k in range(GROUP):
+        pltpu.make_async_copy(late[k], buf.at[k], in_sem).start()
+    pltpu.make_async_copy(buf, buf, in_sem).wait()
+
+    def differs(bit, mine):
+        return 1 - mine if bit else mine
+
+    for r in range(GROUP):
+        ry, rx, rc, _, _ = positions(r)
+        k = dev(differs(ry, y), differs(rx, x), differs(rc, c))
+        start, end = own_start(r) + 2 * GATHERED, own_start(r + 1)
+        for kind, ref in enumerate(outs):
+            lo, hi = max(start, EDGES[kind]), min(end, EDGES[kind + 1])
+            if lo >= hi:
+                continue
+            if is_rows(kind):
+                pltpu.make_async_copy(
+                    buf.at[k, pl.ds(lo - start, hi - lo)], ref.at[pl.ds(lo - EDGES[kind], hi - lo)],
+                    out_sem).start()
+                continue
+            assert ref.shape[1] == COLS
+            for layer in range(ref.shape[0]):
+                base = EDGES[kind] + COLS * layer
+                at, to = max(lo, base), min(hi, base + COLS)
+                if at < to:
+                    def one(rt, z, ref=ref, layer=layer, k=k, n=at - start, col=at - base, tiles=to - at):
+                        pltpu.make_async_copy(
+                            buf.at[k, pl.ds(n, tiles), rt], ref.at[layer, rt, pl.ds(col, tiles)],
+                            out_sem).start()
+                        return z
+                    lax.fori_loop(0, COLS, one, 0)
+    for r in range(GROUP):
+        view = buf.at[r, pl.ds(0, own_start(r + 1) - own_start(r) - 2 * GATHERED)]
+        pltpu.make_async_copy(view, view, out_sem).wait()
+
+
+def out_views(shapes):
+    views = []
+    for kind in range(len(EDGES) - 1):
+        if is_rows(kind):
+            views.append((EDGES[kind + 1] - EDGES[kind],) + TILE)
+        else:
+            views.append((shapes[kind][0], shapes[kind][2] // 8) + TILE)
+    return views
+
+
+def run_unpack(o, kinds, views):
+    bf16, dma, depth = jnp.bfloat16, pltpu.SemaphoreType.DMA, 4
     any_spec = pl.BlockSpec(memory_space=pl.ANY)
-
-    def rows(n):
-        return (n,) + TILE
-
-    def grid(shape):
-        return (shape[0], shape[2] // 8) + TILE
-    views = [rows(e[1]), grid(shapes[1]), grid(shapes[2]), grid(shapes[3]), rows(e[5] - e[4]),
-             grid(shapes[5]), grid(shapes[6]), rows(e[8] - e[7]), rows(4)]
-    dma = pltpu.SemaphoreType.DMA
-    depth = 4
-    outs = pl.pallas_call(
-        unpack_kernel, out_shape=[jax.ShapeDtypeStruct(s, bf16) for s in views],
-        in_specs=[any_spec], out_specs=[any_spec] * len(views),
+    size = sum(math.prod(views[kind]) for kind in kinds)
+    return pl.pallas_call(
+        functools.partial(unpack_kernel, kinds),
+        out_shape=[jax.ShapeDtypeStruct(views[kind], bf16) for kind in kinds],
+        in_specs=[any_spec], out_specs=[any_spec] * len(kinds),
         scratch_shapes=[pltpu.VMEM((depth, COLS) + TILE, bf16), dma((depth,)), dma((depth,))],
+        cost_estimate=pl.CostEstimate(flops=size * 1000, bytes_accessed=size * 4, transcendentals=0),
         compiler_params=pltpu.CompilerParams(vmem_limit_bytes=12 * 2**20),
         name="unpack",
     )(o)
 
+
+def run_late(late, params):
+    bf16, dma, count = jnp.bfloat16, pltpu.SemaphoreType.DMA, len(params)
+    any_spec = pl.BlockSpec(memory_space=pl.ANY)
+    return pl.pallas_call(
+        late_kernel, out_shape=[jax.ShapeDtypeStruct(a.shape, bf16) for a in params],
+        in_specs=[any_spec] * (GROUP + count), out_specs=[any_spec] * count,
+        input_output_aliases={GROUP + n: n for n in range(count)},
+        scratch_shapes=[pltpu.VMEM((GROUP, LATE) + TILE, bf16), dma, dma],
+        compiler_params=pltpu.CompilerParams(vmem_limit_bytes=12 * 2**20),
+        name="unpack_late",
+    )(*late, *params)
+
+
+def to_shapes(outs, shapes):
     def from_rows(a, shape):
         return a.swapaxes(1, 2).reshape(shape)
 
@@ -789,6 +865,10 @@
     return tuple(params)
 
 
+def swap(a, bit):
+    return lax.ppermute(a, "dp", [(r, r ^ bit) for r in range(GROUP)])
+
+
 def solution(mesh):
     group_size = mesh.shape["dp"]
     assert group_size == GROUP
@@ -806,9 +886,25 @@
                  for n, s in enumerate(state)]
 
         g, nrm = run_reduce(pack(grads))
-        *moved, o = run_update(hyper_params, nrm, g, state, tails)
-        o, *moved = lax.optimization_barrier([o] + [a[:SHARE] for a in moved])
-        return run_unpack(o.reshape((-1,) + TILE), shapes) + tuple(moved)
+        *moved, o, own = run_update(hyper_params, nrm, g, state, tails)
+        own, moved[0] = lax.optimization_barrier((own, moved[0][:SHARE]))
+        near = [swap(own, bit) for bit in (2, 4, 6)]
+        first = swap(own, 1)
+        o, *moved = lax.optimization_barrier([o, moved[0]] + [a[:SHARE] for a in moved[1:]])
+        o = o.reshape((-1,) + TILE)
+        views = out_views(shapes)
+        early_kinds, other_kinds = (0, 4, 7, 5), (1, 2, 3, 6, 8)
+        early = run_unpack(o, early_kinds, views)
+        o, near, early = lax.optimization_barrier((o, near, early))
+        cross = [swap(a, 1) for a in near]
+        other = run_unpack(o, other_kinds, views)
+        cross, other = lax.optimization_barrier((cross, other))
+        found = dict(zip(early_kinds + other_kinds, list(early) + list(other)))
+        late = [own, first]
+        for a, b in zip(near, cross):
+            late += [a, b]
+        outs = run_late(late, [found[kind] for kind in range(len(views))])
+        return to_shapes(outs, shapes) + tuple(moved)
 
     in_specs = tuple([P("dp")] * GRAD_COUNT + [P("dp"), P("dp"), P("dp"), P()])
     out_specs = tuple([P()] * GRAD_COUNT + [P("dp"), P("dp"), P("dp")])

time: 1000 us -> 979 us (0.979)
  Pallas kernels: 957 us -> 925 us
    pallas_call x1, Pallas kernels: 304 us -> 268 us  [run_update(): pl.pallas_call(update_kernel, in_specs=[pl.BlockSpec(memory_space=pltpu.S...]
    pallas_call x1 -> x3, Pallas kernels: 46.6 us -> 50.9 us  [the longest x2 46.1 us: run_unpack(): pl.pallas_call(functools.partial(unpack_kernel, kinds), out_shape=[jax.Sh...]
  transfers between devices with their start and end apart: 1 -> 8, of which waited for: 0 -> 1; matrix products, arithmetic and copies ran while one was open for 0% -> 2% of each run, Pallas kernels for 0% -> 5%
where the time goes in v4:
time: 979 us; the launch traced here: 975 us
  Pallas kernels  925 us (94%)
  local copies, waits for them, and re-layouts  37.3 us (4%)
    pallas_call x1, Pallas kernels, run_reduce(): pl.pallas_call(reduce_kernel, out_shape=out_shape, in_specs=[any_spec] *...  606 us
    pallas_call x1, Pallas kernels, run_update(): pl.pallas_call(update_kernel, in_specs=[pl.BlockSpec(memory_space=pltpu.S...  268 us
    pallas_call x2, Pallas kernels, run_unpack(): pl.pallas_call(functools.partial(unpack_kernel, kinds), out_shape=[jax.Sh...  46.1 us
  transfers between devices with their start and end apart: 8, of which 1 were waited for; matrix products, arithmetic and copies ran while one was open for 2% of the time, Pallas kernels for 5%

profile of v4, /device:TPU:0, one launch (start us, length us, event | category | flops | bytes accessed | tf_op | source)
XLA Modules:
  0.0 975.1 jit_solution(10765161289815979087)
XLA Ops:
  0.6 0.9 slice.47
  1.6 0.9 slice.48
  2.5 0.9 slice.49
  3.5 1.3 collective-permute-start
  4.8 0.7 reshape_squeeze.19
  5.5 1.0 reshape_squeeze.18
  6.6 0.8 copy.40
  7.4 605.8 %reduce_scatter.1 = (f32[35712,128]{1,0:T(8,128)}, f32[8,128]{1,0:T(8,128)}, bf16[2,3,2,62,36,8,128]{6,5,4,3,2,1,0:T(8,128)(2,1)}, f32[2,62,36,8,128]{4,3,2,1,0:T(8,128)}) custom-call(bf16[250,36,8,128]{3,2,1,0:T(8,128)(2,1)} %bitcast.87, bf16[6,4,36,8,128]{4,3,2,1,0:T(8,128)(2,1)} %bitcast.98, bf16[6,2,36,8,128]{4,3,2,1,0:T(8,128)(2,1)} %bitcast.100, ...), custom_call_target="tpu_custom_call" | custom-call | tf_op jit(solution)/shard_map/reduce_scatter/pallas_call | solution.py:385
  613.4 1.4 concatenate.19.pt
  614.7 1.4 concatenate.18.vt
  616.1 1.4 concatenate.17.mt
  618.2 268.3 %update_gather.1 = (f32[4497408]{0:T(1024)S(1)}, f32[4497408]{0:T(1024)S(1)}, f32[4497408]{0:T(1024)}, bf16[416,2,36,8,128]{4,3,2,1,0:T(8,128)(2,1)}, bf16[18,36,8,128]{3,2,1,0:T(8,128)(2,1)S(1)}) custom-call(f32[5]{0:T(128)S(1)} %copy-done.1, f32[8,128]{1,0:T(8,128)S(1)} %copy-done, f32[35712,128]{1,0:T(8,128)} %get-tuple-element.61.g_hbm, f32[4483776]{0:T(1024)} %m_hbm.1, ...), custom_call_target="tpu_custom_call" | custom-call | tf_op jit(solution)/shard_map/update_gather/pallas_call | solution.py:654
  886.5 6.6 slice.55
  893.1 1.4 collective-permute-start.4
  894.4 2.0 collective-permute-start.3
  896.6 9.0 slice.56
  905.5 3.3 copy-done.2
  908.8 6.6 slice.57
  915.4 32.8 %unpack.2 = (bf16[250,36,8,128]{3,2,1,0:T(8,128)(2,1)}, bf16[24,36,8,128]{3,2,1,0:T(8,128)(2,1)}, bf16[216,36,8,128]{3,2,1,0:T(8,128)(2,1)}, bf16[6,36,36,8,128]{4,3,2,1,0:T(8,128)(2,1)}) custom-call(bf16[832,36,8,128]{3,2,1,0:T(8,128)(2,1)} %bitcast.85), custom_call_target="tpu_custom_call" | custom-call | flops 26025984000 | bytes 104103936 | tf_op jit(solution)/shard_map/unpack/pallas_call | solution.py:829
  948.2 5.7 collective-permute-done.3.refs_4_
  954.0 0.9 collective-permute-start.5
  955.3 13.3 %unpack.3 = (bf16[6,4,36,8,128]{4,3,2,1,0:T(8,128)(2,1)}, bf16[6,2,36,8,128]{4,3,2,1,0:T(8,128)(2,1)}, bf16[6,2,36,8,128]{4,3,2,1,0:T(8,128)(2,1)}, bf16[6,36,36...) custom-call(bf16[832,36,8,128]{3,2,1,0:T(8,128)(2,1)} %bitcast.86), custom_call_target="tpu_custom_call" | custom-call | flops 9953280000 | bytes 39813120 | tf_op jit(solution)/shard_map/unpack/pallas_call | solution.py:829
  968.7 4.8 unpack_late.1
  973.6 0.8 reshape.91
  (32 shorter events, 2.3 us)
Async XLA Ops:
  3.5 609.8 %collective-permute-start = (f32[110592]{0:T(1024)S(1)}, f32[110592]{0:T(1024)S(1)}, u32[]{:S(2)}, u32[]{:S(2)}) collective-permute-start(f32[110592]{0:T(1024)S(1)} %pad_maximum_fusion), channel_id=1, source_target_pairs={{1,0},{2,1},{3,2},{4,3},{5,4},{6,5},{7,6}} | collective-permute-start | bytes 1327112 | tf_op jit(solution)/shard_map/ppermute | solution.py:883
  7.4 605.9 %slice-start.2 = ((f32[4483776]{0:T(1024)}), f32[23232]{0:T(1024)S(1)}, s32[]{:S(2)}) async-start(f32[4483776]{0:T(1024)} %p_hbm.1), calls=%async_computation.2 | async-start | bytes 188416 | tf_op jit(solution)/shard_map/slice | solution.py:885
  7.4 607.3 %slice-start.1 = ((f32[4483776]{0:T(1024)}), f32[23232]{0:T(1024)S(1)}, s32[]{:S(2)}) async-start(f32[4483776]{0:T(1024)} %v_hbm.1), calls=%async_computation.1 | async-start | bytes 188416 | tf_op jit(solution)/shard_map/slice | solution.py:885
  7.4 608.7 %slice-start = ((f32[4483776]{0:T(1024)}), f32[23232]{0:T(1024)S(1)}, s32[]{:S(2)}) async-start(f32[4483776]{0:T(1024)} %m_hbm.1), calls=%async_computation | async-start | bytes 188416 | tf_op jit(solution)/shard_map/slice | solution.py:885
  7.4 610.1 %copy-start.1 = (f32[5]{0:T(128)S(1)}, f32[5]{0:T(128)}, u32[]{:S(2)}) copy-start(f32[5]{0:T(128)} %hyper_ref.1) | copy-start | bytes 64
  617.5 0.7 copy-start
  893.1 55.2 %collective-permute-start.4 = (bf16[18,36,8,128]{3,2,1,0:T(8,128)(2,1)S(1)}, bf16[18,36,8,128]{3,2,1,0:T(8,128)(2,1)S(1)}, u32[]{:S(2)}, u32[]{:S(2)}) collective-permute-start(bf16[18,36,8,128]{3,2,1,0:T(8,128)(2,1)S(1)} %get-tuple-element.64.refs_0_), channel_id=1, source_target_pairs={{0,6},{1,7},{2,4},{3,5},{4,2},{5,3},{6,0},{7,1}} | collective-permute-start | bytes 3981320 | tf_op jit(solution)/shard_map/ppermute | solution.py:869
  894.4 59.5 %collective-permute-start.3 = (bf16[18,36,8,128]{3,2,1,0:T(8,128)(2,1)S(1)}, bf16[18,36,8,128]{3,2,1,0:T(8,128)(2,1)S(1)}, u32[]{:S(2)}, u32[]{:S(2)}) collective-permute-start(bf16[18,36,8,128]{3,2,1,0:T(8,128)(2,1)S(1)} %get-tuple-element.64.refs_0_), channel_id=1, source_target_pairs={{0,4},{1,5},{2,6},{3,7},{4,0},{5,1},{6,2},{7,3}} | collective-permute-start | bytes 3981320 | tf_op jit(solution)/shard_map/ppermute | solution.py:869
  896.5 57.5 %collective-permute-start.2 = (bf16[18,36,8,128]{3,2,1,0:T(8,128)(2,1)S(1)}, bf16[18,36,8,128]{3,2,1,0:T(8,128)(2,1)S(1)}, u32[]{:S(2)}, u32[]{:S(2)}) collective-permute-start(bf16[18,36,8,128]{3,2,1,0:T(8,128)(2,1)S(1)} %get-tuple-element.64.refs_0_), channel_id=1, source_target_pairs={{0,2},{1,3},{2,0},{3,1},{4,6},{5,7},{6,4},{7,5}} | collective-permute-start | bytes 3981320 | tf_op jit(solution)/shard_map/ppermute | solution.py:869
  896.6 12.3 %copy-start.2 = (f32[4497408]{0:T(1024)S(1)}, f32[4497408]{0:T(1024)}, u32[]{:S(2)}) copy-start(f32[4497408]{0:T(1024)} %get-tuple-element.68) | copy-start | bytes 53968900
  954.0 14.7 %collective-permute-start.5 = (bf16[18,36,8,128]{3,2,1,0:T(8,128)(2,1)S(1)}, bf16[18,36,8,128]{3,2,1,0:T(8,128)(2,1)S(1)}, u32[]{:S(2)}, u32[]{:S(2)}) collective-permute-start(bf16[18,36,8,128]{3,2,1,0:T(8,128)(2,1)S(1)} %collective-permute-done.2.refs_2_), channel_id=1, source_target_pairs={{0,1},{1,0},{2,3},{3,2},{4,5},{5,4},{6,7},{7,6}} | collective-permute-start | bytes 3981320 | tf_op jit(solution)/shard_map/ppermute | solution.py:869
  954.8 13.9 %collective-permute-start.6 = (bf16[18,36,8,128]{3,2,1,0:T(8,128)(2,1)S(1)}, bf16[18,36,8,128]{3,2,1,0:T(8,128)(2,1)S(1)}, u32[]{:S(2)}, u32[]{:S(2)}) collective-permute-start(bf16[18,36,8,128]{3,2,1,0:T(8,128)(2,1)S(1)} %collective-permute-done.3.refs_4_), channel_id=1, source_target_pairs={{0,1},{1,0},{2,3},{3,2},{4,5},{5,4},{6,7},{7,6}} | collective-permute-start | bytes 3981320 | tf_op jit(solution)/shard_map/ppermute | solution.py:869
  954.8 13.9 %collective-permute-start.7 = (bf16[18,36,8,128]{3,2,1,0:T(8,128)(2,1)S(1)}, bf16[18,36,8,128]{3,2,1,0:T(8,128)(2,1)S(1)}, u32[]{:S(2)}, u32[]{:S(2)}) collective-permute-start(bf16[18,36,8,128]{3,2,1,0:T(8,128)(2,1)S(1)} %collective-permute-done.4.refs_6_), channel_id=1, source_target_pairs={{0,1},{1,0},{2,3},{3,2},{4,5},{5,4},{6,7},{7,6}} | collective-permute-start | bytes 3981320 | tf_op jit(solution)/shard_map/ppermute | solution.py:869
  955.3 13.4 %collective-permute-start.1 = (bf16[18,36,8,128]{3,2,1,0:T(8,128)(2,1)S(1)}, bf16[18,36,8,128]{3,2,1,0:T(8,128)(2,1)S(1)}, u32[]{:S(2)}, u32[]{:S(2)}) collective-permute-start(bf16[18,36,8,128]{3,2,1,0:T(8,128)(2,1)S(1)} %get-tuple-element.64.refs_0_), channel_id=1, source_target_pairs={{0,1},{1,0},{2,3},{3,2},{4,5},{5,4},{6,7},{7,6}} | collective-permute-start | bytes 3981320 | tf_op jit(solution)/shard_map/ppermute | solution.py:869

commit v5 on v4

--- a/solution.py
+++ b/solution.py
@@ -27,7 +27,7 @@
 COVER = 2 * HALF
 CH = 2
 CHUNKS = HALF // CH
-AHEAD = 3
+AHEAD = 4
 SLOTS = 8
 OWN = 122
 OWN_HALF = OWN // 2
@@ -37,8 +37,8 @@
 TAIL_BLOCKS = 6
 TILE = (36, 8, 128)
 COLS = 36
-NEAR_LAG = 2
-FAR_LAG = 4
+NEAR_LAG = 5
+FAR_LAG = 9
 PART = 2
 DECAY_LEN = 970 * BLK
 

time: 979 us -> 972 us (level)
  transfers between devices with their start and end apart: 8 -> 8, of which waited for: 1 -> 2; matrix products, arithmetic and copies ran while one was open for 2% -> 2% of each run, Pallas kernels for 5% -> 5%
where the time goes in v5:
time: 972 us; the launch traced here: 968 us
  Pallas kernels  918 us (94%)
  local copies, waits for them, and re-layouts  37.3 us (4%)
    pallas_call x1, Pallas kernels, run_reduce(): pl.pallas_call(reduce_kernel, out_shape=out_shape, in_specs=[any_spec] *...  606 us
    pallas_call x1, Pallas kernels, run_update(): pl.pallas_call(update_kernel, in_specs=[pl.BlockSpec(memory_space=pltpu.S...  261 us
    pallas_call x2, Pallas kernels, run_unpack(): pl.pallas_call(functools.partial(unpack_kernel, kinds), out_shape=[jax.Sh...  46.1 us
  transfers between devices with their start and end apart: 8, of which 2 were waited for; matrix products, arithmetic and copies ran while one was open for 2% of the time, Pallas kernels for 5%

profile of v5, /device:TPU:0, one launch (start us, length us, event | category | flops | bytes accessed | tf_op | source)
XLA Modules:
  0.0 967.7 jit_solution(8264782153476287466)
XLA Ops:
  0.6 0.9 slice.47
  1.6 0.9 slice.48
  2.5 0.9 slice.49
  3.5 1.3 collective-permute-start
  4.8 0.7 reshape_squeeze.19
  5.5 1.0 reshape_squeeze.18
  6.6 0.8 copy.40
  7.4 605.8 %reduce_scatter.1 = (f32[35712,128]{1,0:T(8,128)}, f32[8,128]{1,0:T(8,128)}, bf16[2,3,2,62,36,8,128]{6,5,4,3,2,1,0:T(8,128)(2,1)}, f32[2,62,36,8,128]{4,3,2,1,0:T(8,128)}) custom-call(bf16[250,36,8,128]{3,2,1,0:T(8,128)(2,1)} %bitcast.87, bf16[6,4,36,8,128]{4,3,2,1,0:T(8,128)(2,1)} %bitcast.98, bf16[6,2,36,8,128]{4,3,2,1,0:T(8,128)(2,1)} %bitcast.100, ...), custom_call_target="tpu_custom_call" | custom-call | tf_op jit(solution)/shard_map/reduce_scatter/pallas_call | solution.py:385
  613.4 1.4 concatenate.19.pt
  614.7 1.4 concatenate.18.vt
  616.1 1.4 concatenate.17.mt
  617.5 0.7 copy-done
  618.2 261.3 %update_gather.1 = (f32[4497408]{0:T(1024)S(1)}, f32[4497408]{0:T(1024)S(1)}, f32[4497408]{0:T(1024)}, bf16[416,2,36,8,128]{4,3,2,1,0:T(8,128)(2,1)}, bf16[18,36,8,128]{3,2,1,0:T(8,128)(2,1)S(1)}) custom-call(f32[5]{0:T(128)S(1)} %copy-done.1, f32[8,128]{1,0:T(8,128)S(1)} %copy-done, f32[35712,128]{1,0:T(8,128)} %get-tuple-element.61.g_hbm, f32[4483776]{0:T(1024)} %m_hbm.1, ...), custom_call_target="tpu_custom_call" | custom-call | tf_op jit(solution)/shard_map/update_gather/pallas_call | solution.py:654
  879.5 6.6 slice.55
  886.1 1.7 collective-permute-start.4
  887.7 1.2 collective-permute-start.3
  889.5 9.0 slice.56
  898.5 3.3 copy-done.2
  901.8 6.6 slice.57
  908.4 32.8 %unpack.2 = (bf16[250,36,8,128]{3,2,1,0:T(8,128)(2,1)}, bf16[24,36,8,128]{3,2,1,0:T(8,128)(2,1)}, bf16[216,36,8,128]{3,2,1,0:T(8,128)(2,1)}, bf16[6,36,36,8,128]{4,3,2,1,0:T(8,128)(2,1)}) custom-call(bf16[832,36,8,128]{3,2,1,0:T(8,128)(2,1)} %bitcast.85), custom_call_target="tpu_custom_call" | custom-call | flops 26025984000 | bytes 104103936 | tf_op jit(solution)/shard_map/unpack/pallas_call | solution.py:829
  941.2 5.2 collective-permute-done.3.refs_4_
  947.9 13.3 %unpack.3 = (bf16[6,4,36,8,128]{4,3,2,1,0:T(8,128)(2,1)}, bf16[6,2,36,8,128]{4,3,2,1,0:T(8,128)(2,1)}, bf16[6,2,36,8,128]{4,3,2,1,0:T(8,128)(2,1)}, bf16[6,36,36...) custom-call(bf16[832,36,8,128]{3,2,1,0:T(8,128)(2,1)} %bitcast.86), custom_call_target="tpu_custom_call" | custom-call | flops 9953280000 | bytes 39813120 | tf_op jit(solution)/shard_map/unpack/pallas_call | solution.py:829
  961.3 4.8 unpack_late.1
  966.2 0.8 reshape.91
  (32 shorter events, 3.1 us)
Async XLA Ops:
  3.5 609.8 %collective-permute-start = (f32[110592]{0:T(1024)S(1)}, f32[110592]{0:T(1024)S(1)}, u32[]{:S(2)}, u32[]{:S(2)}) collective-permute-start(f32[110592]{0:T(1024)S(1)} %pad_maximum_fusion), channel_id=1, source_target_pairs={{1,0},{2,1},{3,2},{4,3},{5,4},{6,5},{7,6}} | collective-permute-start | bytes 1327112 | tf_op jit(solution)/shard_map/ppermute | solution.py:883
  7.4 605.9 %slice-start.2 = ((f32[4483776]{0:T(1024)}), f32[23232]{0:T(1024)S(1)}, s32[]{:S(2)}) async-start(f32[4483776]{0:T(1024)} %p_hbm.1), calls=%async_computation.2 | async-start | bytes 188416 | tf_op jit(solution)/shard_map/slice | solution.py:885
  7.4 607.3 %slice-start.1 = ((f32[4483776]{0:T(1024)}), f32[23232]{0:T(1024)S(1)}, s32[]{:S(2)}) async-start(f32[4483776]{0:T(1024)} %v_hbm.1), calls=%async_computation.1 | async-start | bytes 188416 | tf_op jit(solution)/shard_map/slice | solution.py:885
  7.4 608.7 %slice-start = ((f32[4483776]{0:T(1024)}), f32[23232]{0:T(1024)S(1)}, s32[]{:S(2)}) async-start(f32[4483776]{0:T(1024)} %m_hbm.1), calls=%async_computation | async-start | bytes 188416 | tf_op jit(solution)/shard_map/slice | solution.py:885
  7.4 610.1 %copy-start.1 = (f32[5]{0:T(128)S(1)}, f32[5]{0:T(128)}, u32[]{:S(2)}) copy-start(f32[5]{0:T(128)} %hyper_ref.1) | copy-start | bytes 64
  617.5 0.7 copy-start
  886.1 55.2 %collective-permute-start.4 = (bf16[18,36,8,128]{3,2,1,0:T(8,128)(2,1)S(1)}, bf16[18,36,8,128]{3,2,1,0:T(8,128)(2,1)S(1)}, u32[]{:S(2)}, u32[]{:S(2)}) collective-permute-start(bf16[18,36,8,128]{3,2,1,0:T(8,128)(2,1)S(1)} %get-tuple-element.64.refs_0_), channel_id=1, source_target_pairs={{0,6},{1,7},{2,4},{3,5},{4,2},{5,3},{6,0},{7,1}} | collective-permute-start | bytes 3981320 | tf_op jit(solution)/shard_map/ppermute | solution.py:869
  887.7 58.7 %collective-permute-start.3 = (bf16[18,36,8,128]{3,2,1,0:T(8,128)(2,1)S(1)}, bf16[18,36,8,128]{3,2,1,0:T(8,128)(2,1)S(1)}, u32[]{:S(2)}, u32[]{:S(2)}) collective-permute-start(bf16[18,36,8,128]{3,2,1,0:T(8,128)(2,1)S(1)} %get-tuple-element.64.refs_0_), channel_id=1, source_target_pairs={{0,4},{1,5},{2,6},{3,7},{4,0},{5,1},{6,2},{7,3}} | collective-permute-start | bytes 3981320 | tf_op jit(solution)/shard_map/ppermute | solution.py:869
  889.0 57.9 %collective-permute-start.2 = (bf16[18,36,8,128]{3,2,1,0:T(8,128)(2,1)S(1)}, bf16[18,36,8,128]{3,2,1,0:T(8,128)(2,1)S(1)}, u32[]{:S(2)}, u32[]{:S(2)}) collective-permute-start(bf16[18,36,8,128]{3,2,1,0:T(8,128)(2,1)S(1)} %get-tuple-element.64.refs_0_), channel_id=1, source_target_pairs={{0,2},{1,3},{2,0},{3,1},{4,6},{5,7},{6,4},{7,5}} | collective-permute-start | bytes 3981320 | tf_op jit(solution)/shard_map/ppermute | solution.py:869
  889.5 12.3 %copy-start.2 = (f32[4497408]{0:T(1024)S(1)}, f32[4497408]{0:T(1024)}, u32[]{:S(2)}) copy-start(f32[4497408]{0:T(1024)} %get-tuple-element.68) | copy-start | bytes 53968900
  946.9 14.4 %collective-permute-start.5 = (bf16[18,36,8,128]{3,2,1,0:T(8,128)(2,1)S(1)}, bf16[18,36,8,128]{3,2,1,0:T(8,128)(2,1)S(1)}, u32[]{:S(2)}, u32[]{:S(2)}) collective-permute-start(bf16[18,36,8,128]{3,2,1,0:T(8,128)(2,1)S(1)} %collective-permute-done.2.refs_2_), channel_id=1, source_target_pairs={{0,1},{1,0},{2,3},{3,2},{4,5},{5,4},{6,7},{7,6}} | collective-permute-start | bytes 3981320 | tf_op jit(solution)/shard_map/ppermute | solution.py:869
  946.9 14.4 %collective-permute-start.6 = (bf16[18,36,8,128]{3,2,1,0:T(8,128)(2,1)S(1)}, bf16[18,36,8,128]{3,2,1,0:T(8,128)(2,1)S(1)}, u32[]{:S(2)}, u32[]{:S(2)}) collective-permute-start(bf16[18,36,8,128]{3,2,1,0:T(8,128)(2,1)S(1)} %collective-permute-done.3.refs_4_), channel_id=1, source_target_pairs={{0,1},{1,0},{2,3},{3,2},{4,5},{5,4},{6,7},{7,6}} | collective-permute-start | bytes 3981320 | tf_op jit(solution)/shard_map/ppermute | solution.py:869
  947.4 13.9 %collective-permute-start.7 = (bf16[18,36,8,128]{3,2,1,0:T(8,128)(2,1)S(1)}, bf16[18,36,8,128]{3,2,1,0:T(8,128)(2,1)S(1)}, u32[]{:S(2)}, u32[]{:S(2)}) collective-permute-start(bf16[18,36,8,128]{3,2,1,0:T(8,128)(2,1)S(1)} %collective-permute-done.4.refs_6_), channel_id=1, source_target_pairs={{0,1},{1,0},{2,3},{3,2},{4,5},{5,4},{6,7},{7,6}} | collective-permute-start | bytes 3981320 | tf_op jit(solution)/shard_map/ppermute | solution.py:869
  947.4 13.9 %collective-permute-start.1 = (bf16[18,36,8,128]{3,2,1,0:T(8,128)(2,1)S(1)}, bf16[18,36,8,128]{3,2,1,0:T(8,128)(2,1)S(1)}, u32[]{:S(2)}, u32[]{:S(2)}) collective-permute-start(bf16[18,36,8,128]{3,2,1,0:T(8,128)(2,1)S(1)} %get-tuple-element.64.refs_0_), channel_id=1, source_target_pairs={{0,1},{1,0},{2,3},{3,2},{4,5},{5,4},{6,7},{7,6}} | collective-permute-start | bytes 3981320 | tf_op jit(solution)/shard_map/ppermute | solution.py:869
